TPU v7x, 32 devices: a whole 2x2x4 slice. The times are simulated.
32 devices in a mesh: grp: 4 (over y, x), tile: 8 (over z, core).
Axes of the slice: x: 2, y: 2, z: 4, core: 2. Of those that a mesh axis runs over, the one named last changes fastest.
Arguments:
- base_rhs: float32 [1024, 4096], P('grp', 'tile'), may hold values from -6 to 6
- depth: float32 [1024, 4096], P('grp', 'tile'), may hold values from 0.25 to 2
- ssh_prev: float32 [1024, 4096], P('grp', 'tile'), may hold values from -6 to 6
- currents: float32 [2, 1024, 4096], P(None, 'grp', 'tile'), may hold values from -3 to 3
- land_blocks: int32 [128, 512], P('grp', 'tile'), may hold values 0 or 1
- ice_thick: float32 [2, 256, 4096], P(None, 'grp', 'tile'), may hold values from 0.25 to 4
- ice_blocks: int32 [2, 32, 512], P(None, 'grp', 'tile'), may hold values 0 or 1
- ice_vel: float32 [2, 2, 256, 4096], P(None, None, 'grp', 'tile'), may hold values from -3 to 3
- ice_stress: float32 [3, 2, 256, 4096], P(None, None, 'grp', 'tile'), may hold values from -5 to 5
- wind: float32 [2, 2, 256, 4096], P(None, None, 'grp', 'tile'), may hold values from -6 to 6
Outputs:
- ssh: float32 [1024, 4096], P('grp', 'tile')
- ice_vel_out: float32 [2, 2, 256, 4096], P(None, None, 'grp', 'tile')
- ice_stress_out: float32 [3, 2, 256, 4096], P(None, None, 'grp', 'tile')
All inputs are finite; a program needn't handle non-finite values. No bound on the sum of `land_blocks` or of `ice_blocks` on one device may be relied on, other than what follows from the above.
Results may differ from a plain program's by a relative error of at most 0.0001.
Values sent between devices are 32-bit elements; how exact they have to be, the bound alone decides.
A program may use at most 64 MiB of HBM per device.

v0:
```python
import jax
import jax.numpy as jnp
from jax import lax
from jax.sharding import PartitionSpec as P

BS = 8
NSUB = 8
ITERS = 3


DAMP = 0.05
RELAX = 0.2
STRENGTH = 0.5
DRAG = 1.0
STEP = 0.5


def extended(array, sides, width):
    for axis, dim in sides:
        devices, length = (lax.axis_size(axis), array.shape[dim])
        up = [(i, (i + 1) % devices) for i in range(devices - 1)]
        down = [(j, i) for i, j in up]
        last = lax.slice_in_dim(array, length - width, length, axis=dim)
        first = lax.slice_in_dim(array, 0, width, axis=dim)
        before = lax.ppermute(last, axis, up)
        after = lax.ppermute(first, axis, down)
        array = jnp.concatenate([before, array, after], axis=dim)
    return array


def passed_along(array, axis, by):
    devices = lax.axis_size(axis)
    pairs = [(i, i + by) for i in range(devices) if 0 <= i + by < devices]
    return lax.ppermute(array, axis, pairs)


def strain_rates(u_pad, v_pad):
    du_dx = u_pad[..., 1:, :-1] - u_pad[..., :-1, :-1]
    du_dy = u_pad[..., :-1, 1:] - u_pad[..., :-1, :-1]
    dv_dx = v_pad[..., 1:, :-1] - v_pad[..., :-1, :-1]
    dv_dy = v_pad[..., :-1, 1:] - v_pad[..., :-1, :-1]
    return (du_dx + dv_dy, du_dx - dv_dy, du_dy + dv_dx)


def relax_stress(previous, strength, div_rate, tens_rate, shear_rate):
    deformation = jnp.sqrt(
        div_rate * div_rate + tens_rate * tens_rate + shear_rate * shear_rate + 1.0
    )
    relax_scale = 1.0 / (1.0 + RELAX)
    div_part = (previous[0] + RELAX * strength * (div_rate / deformation - 1.0)) * relax_scale
    tens_part = (previous[1] + RELAX * strength * tens_rate / deformation) * relax_scale
    shear_part = (previous[2] + RELAX * strength * shear_rate / deformation) * relax_scale
    return jnp.stack([div_part, tens_part, shear_part])


def along_rows(field):
    return field[..., 1:, 1:] - field[..., :-1, 1:]


def along_cols(field):
    return field[..., 1:, 1:] - field[..., 1:, :-1]


def stress_force(stress_pad):
    force_x = 0.5 * along_rows(stress_pad[0] + stress_pad[1]) + along_cols(stress_pad[2])
    force_y = 0.5 * along_cols(stress_pad[0] - stress_pad[1]) + along_rows(stress_pad[2])
    return jnp.stack([force_x, force_y])


def momentum(velocity, force, ice_mass, ice_cover, wind, ocean_flow):
    return (
        ice_cover
        * (ice_mass * velocity + STEP * (force + wind + DRAG * ocean_flow))
        / (ice_mass + STEP * DRAG)
    )


def face_weights(depth_pad):
    centre = depth_pad[1:-1, 1:-1]
    return (
        centre * depth_pad[2:, 1:-1],
        centre * depth_pad[:-2, 1:-1],
        centre * depth_pad[1:-1, 2:],
        centre * depth_pad[1:-1, :-2],
    )


def apply_operator(field_pad, weights):
    field = field_pad[1:-1, 1:-1]
    north_weight, south_weight, east_weight, west_weight = weights
    return (
        DAMP * field
        + north_weight * (field - field_pad[2:, 1:-1])
        + south_weight * (field - field_pad[:-2, 1:-1])
        + east_weight * (field - field_pad[1:-1, 2:])
        + west_weight * (field - field_pad[1:-1, :-2])
    )


def expand(blocks):
    return jnp.repeat(jnp.repeat(blocks, BS, axis=-2), BS, axis=-1).astype(jnp.float32)


def operate(field, weights):
    field_pad = extended(field, (("grp", 0), ("tile", 1)), 1)
    return apply_operator(field_pad, weights)


def forward_edges(velocity):
    row_in = passed_along(velocity[:, :, :1, :], "grp", -1)
    col_in = passed_along(velocity[:, :, :, :1], "tile", -1)
    taller = jnp.concatenate([velocity, row_in], axis=2)
    col_tall = jnp.pad(col_in, ((0, 0), (0, 0), (0, 1), (0, 0)))
    return jnp.concatenate([taller, col_tall], axis=3)


def backward_edges(stress):
    row_in = passed_along(stress[:, :, -1:, :], "grp", 1)
    col_in = passed_along(stress[:, :, :, -1:], "tile", 1)
    taller = jnp.concatenate([row_in, stress], axis=2)
    col_tall = jnp.pad(col_in, ((0, 0), (0, 0), (1, 0), (0, 0)))
    return jnp.concatenate([col_tall, taller], axis=3)


def pair_sums(residual, precond, applied):
    return lax.psum((jnp.sum(residual * precond), jnp.sum(precond * applied)), ("grp", "tile"))


def shards(
    base_rhs,
    depth,
    ssh_prev,
    currents,
    land_blocks,
    ice_thick,
    ice_blocks,
    ice_vel,
    ice_stress,
    wind,
):
    groups = lax.axis_size("grp")
    grp_index = lax.axis_index("grp")
    ocean_cols = base_rhs.shape[1]
    ice_rows = ice_thick.shape[1]
    cap_rows = ice_rows * groups
    wet_cells = expand(land_blocks)
    ice_cover = expand(ice_blocks)
    at_north = (grp_index == 0).astype(jnp.float32)
    at_south = (grp_index == groups - 1).astype(jnp.float32)
    outgoing = jnp.stack([currents * at_north, currents * at_south], axis=1)
    outgoing = outgoing.reshape(2, 2, groups, ice_rows, ocean_cols)
    incoming = lax.all_to_all(outgoing, "grp", split_axis=2, concat_axis=2, tiled=True)
    ocean_flow = jnp.sum(incoming, axis=2)
    strength = STRENGTH * ice_thick * ice_cover
    ice_mass = ice_thick * ice_cover + 1.0
    velocity = ice_vel
    stress = ice_stress
    for subcycle in range(NSUB):
        vel_pad = forward_edges(velocity)
        div_rate, tens_rate, shear_rate = strain_rates(vel_pad[0], vel_pad[1])
        stress = relax_stress(stress, strength, div_rate, tens_rate, shear_rate)
        stress_pad = backward_edges(stress)
        velocity = momentum(
            velocity, stress_force(stress_pad), ice_mass, ice_cover, wind, ocean_flow
        )
    ice_drag = DRAG * ice_cover * (velocity - ocean_flow)
    empty_slot = jnp.zeros_like(ice_drag[:, 0])
    parcel = jnp.stack([ice_drag[:, 0]] + [empty_slot] * (groups - 2) + [ice_drag[:, 1]], axis=1)
    returned = lax.all_to_all(parcel, "grp", split_axis=1, concat_axis=1, tiled=True).reshape(
        2, cap_rows, ocean_cols
    )
    ocean_drag = jnp.where(
        grp_index == 0, returned, jnp.where(grp_index == groups - 1, returned, 0.0)
    )
    forcing_pad = extended(
        jnp.stack([ocean_drag[0], ocean_drag[1], depth * wet_cells]), (("grp", 1), ("tile", 2)), 1
    )
    spread = (
        forcing_pad[0, 1:-1, 1:-1]
        - forcing_pad[0, :-2, 1:-1]
        + (forcing_pad[1, 1:-1, 1:-1] - forcing_pad[1, 1:-1, :-2])
    )
    forcing = wet_cells * (base_rhs + spread)
    weights = face_weights(forcing_pad[2])
    diagonal = DAMP + weights[0] + weights[1] + weights[2] + weights[3]
    solution = ssh_prev
    residual = forcing - operate(solution, weights)
    precond = residual / diagonal
    applied = operate(precond, weights)
    precond_norm, curvature_sum = pair_sums(residual, precond, applied)
    step_size = precond_norm / curvature_sum
    direction = precond
    search_image = applied
    for iteration in range(ITERS):
        solution = solution + step_size * direction
        residual = residual - step_size * search_image
        if iteration + 1 < ITERS:
            precond = residual / diagonal
            applied = operate(precond, weights)
            norm_next, curvature_sum = pair_sums(residual, precond, applied)
            beta_ratio = norm_next / precond_norm
            step_size = norm_next / (curvature_sum - beta_ratio * norm_next / step_size)
            direction = precond + beta_ratio * direction
            search_image = applied + beta_ratio * search_image
            precond_norm = norm_next
    return (solution, velocity, stress)


def solution(mesh):
    return jax.shard_map(
        shards,
        mesh=mesh,
        in_specs=(
            P("grp", "tile"),
            P("grp", "tile"),
            P("grp", "tile"),
            P(None, "grp", "tile"),
            P("grp", "tile"),
            P(None, "grp", "tile"),
            P(None, "grp", "tile"),
            P(None, None, "grp", "tile"),
            P(None, None, "grp", "tile"),
            P(None, None, "grp", "tile"),
        ),
        out_specs=(P("grp", "tile"), P(None, None, "grp", "tile"), P(None, None, "grp", "tile")),
        check_vma=False,
    )
```

profile of v0, /device:TPU:0, one launch (start us, length us, event | category | flops | bytes accessed | tf_op | source)
XLA Modules:
  0.0 449.4 jit_solution(3022196357651030177)
XLA Ops:
  5.0 1.5 broadcast_multiply_fusion.1
  6.7 1.6 copy.184
  8.3 6.5 %all-to-all-start = ((f32[2,2,4,64,512]{4,3,0,1,2:T(8,128)}), f32[2,2,4,64,512]{4,3,0,1,2:T(8,128)}, u32[]{:S(2)}, u32[]{:S(2)}) async-start(f32[2,2,4,64,512]{4,3,0,1,2:T(8,128)} %copy.184), calls=%async_computation | async-start | bytes 4194304 | tf_op jit(solution)/shard_map/all_to_all | solution.py:152
  17.2 3.9 collective-permute-start.3
  21.2 2.5 collective-permute-start.2
  23.7 15.0 %collective-permute-done.3 = f32[3,2,1,512]{3,1,2,0:T(2,128)S(1)} collective-permute-done((f32[3,2,1,512]{3,1,2,0:T(2,128)S(1)}, f32[3,2,1,512]{3,1,2,0:T(2,128)S(1)}, u32[]{:S(2)}, u32[]{:S(2)}) %collective-permute-start.3) | collective-permute-done | bytes 12320 | tf_op jit(solution)/shard_map/ppermute | solution.py:34
  40.4 1.8 all-to-all-done
  42.2 1.9 reduce_sum.63
  44.1 1.4 fusion.63
  45.5 1.3 collective-permute-start.4
  46.8 1.3 collective-permute-start.5
  48.1 2.9 collective-permute-done.4
  51.9 3.8 collective-permute-start.7
  55.9 4.8 %collective-permute-start.6 = (f32[3,2,64,1]{3,2,1,0:T(8,128)S(1)}, f32[3,2,64,1]{3,2,1,0:T(8,128)S(1)}, u32[]{:S(2)}, u32[]{:S(2)}) collective-permute-start(f32[3,2,64,1]{3,2,1,0:T(8,128)S(1)} %pad_maximum_fusion.52), channel_id=1, source_target_pairs={{0,1},{1,2},{2,3},{3,4},{4,5},{5,6},{6,7},{8,9},{9,10},{10,11},{11... | collective-permute-start | bytes 4616 | tf_op jit(solution)/shard_map/ppermute | solution.py:34
  63.0 1.3 collective-permute-start.8
  65.6 3.4 collective-permute-done.8
  69.9 4.8 %collective-permute-start.11 = (f32[3,2,1,512]{3,1,2,0:T(2,128)S(1)}, f32[3,2,1,512]{3,1,2,0:T(2,128)S(1)}, u32[]{:S(2)}, u32[]{:S(2)}) collective-permute-start(f32[3,2,1,512]{3,1,2,0:T(2,128)S(1)} %copy.198), channel_id=1, source_target_pairs={{0,8},{8,16},{16,24},{1,9},{9,17},{17,25},{2,10},{10,18},{18,26},{... | collective-permute-start | bytes 36872 | tf_op jit(solution)/shard_map/ppermute | solution.py:34
  74.8 5.9 %collective-permute-start.10 = (f32[3,2,64,1]{3,2,1,0:T(8,128)S(1)}, f32[3,2,64,1]{3,2,1,0:T(8,128)S(1)}, u32[]{:S(2)}, u32[]{:S(2)}) collective-permute-start(f32[3,2,64,1]{3,2,1,0:T(8,128)S(1)} %pad_maximum_fusion.51), channel_id=1, source_target_pairs={{0,1},{1,2},{2,3},{3,4},{4,5},{5,6},{6,7},{8,9},{9,10},{10,11},{11... | collective-permute-start | bytes 4616 | tf_op jit(solution)/shard_map/ppermute | solution.py:34
  85.6 3.8 collective-permute-done.12
  90.3 4.8 %collective-permute-start.15 = (f32[3,2,1,512]{3,1,2,0:T(2,128)S(1)}, f32[3,2,1,512]{3,1,2,0:T(2,128)S(1)}, u32[]{:S(2)}, u32[]{:S(2)}) collective-permute-start(f32[3,2,1,512]{3,1,2,0:T(2,128)S(1)} %copy.205), channel_id=1, source_target_pairs={{0,8},{8,16},{16,24},{1,9},{9,17},{17,25},{2,10},{10,18},{18,26},{... | collective-permute-start | bytes 36872 | tf_op jit(solution)/shard_map/ppermute | solution.py:34
  95.3 5.9 %collective-permute-start.14 = (f32[3,2,64,1]{3,2,1,0:T(8,128)S(1)}, f32[3,2,64,1]{3,2,1,0:T(8,128)S(1)}, u32[]{:S(2)}, u32[]{:S(2)}) collective-permute-start(f32[3,2,64,1]{3,2,1,0:T(8,128)S(1)} %pad_maximum_fusion.50), channel_id=1, source_target_pairs={{0,1},{1,2},{2,3},{3,4},{4,5},{5,6},{6,7},{8,9},{9,10},{10,11},{11... | collective-permute-start | bytes 4616 | tf_op jit(solution)/shard_map/ppermute | solution.py:34
  104.8 1.5 collective-permute-start.17
  106.3 3.6 collective-permute-done.16
  110.8 4.8 %collective-permute-start.19 = (f32[3,2,1,512]{3,1,2,0:T(2,128)S(1)}, f32[3,2,1,512]{3,1,2,0:T(2,128)S(1)}, u32[]{:S(2)}, u32[]{:S(2)}) collective-permute-start(f32[3,2,1,512]{3,1,2,0:T(2,128)S(1)} %copy.212), channel_id=1, source_target_pairs={{0,8},{8,16},{16,24},{1,9},{9,17},{17,25},{2,10},{10,18},{18,26},{... | collective-permute-start | bytes 36872 | tf_op jit(solution)/shard_map/ppermute | solution.py:34
  115.7 5.9 %collective-permute-start.18 = (f32[3,2,64,1]{3,2,1,0:T(8,128)S(1)}, f32[3,2,64,1]{3,2,1,0:T(8,128)S(1)}, u32[]{:S(2)}, u32[]{:S(2)}) collective-permute-start(f32[3,2,64,1]{3,2,1,0:T(8,128)S(1)} %pad_maximum_fusion.49), channel_id=1, source_target_pairs={{0,1},{1,2},{2,3},{3,4},{4,5},{5,6},{6,7},{8,9},{9,10},{10,11},{11... | collective-permute-start | bytes 4616 | tf_op jit(solution)/shard_map/ppermute | solution.py:34
  126.5 3.8 collective-permute-done.20
  131.2 4.8 %collective-permute-start.23 = (f32[3,2,1,512]{3,1,2,0:T(2,128)S(1)}, f32[3,2,1,512]{3,1,2,0:T(2,128)S(1)}, u32[]{:S(2)}, u32[]{:S(2)}) collective-permute-start(f32[3,2,1,512]{3,1,2,0:T(2,128)S(1)} %copy.219), channel_id=1, source_target_pairs={{0,8},{8,16},{16,24},{1,9},{9,17},{17,25},{2,10},{10,18},{18,26},{... | collective-permute-start | bytes 36872 | tf_op jit(solution)/shard_map/ppermute | solution.py:34
  136.1 5.9 %collective-permute-start.22 = (f32[3,2,64,1]{3,2,1,0:T(8,128)S(1)}, f32[3,2,64,1]{3,2,1,0:T(8,128)S(1)}, u32[]{:S(2)}, u32[]{:S(2)}) collective-permute-start(f32[3,2,64,1]{3,2,1,0:T(8,128)S(1)} %pad_maximum_fusion.48), channel_id=1, source_target_pairs={{0,1},{1,2},{2,3},{3,4},{4,5},{5,6},{6,7},{8,9},{9,10},{10,11},{11... | collective-permute-start | bytes 4616 | tf_op jit(solution)/shard_map/ppermute | solution.py:34
  147.0 3.8 collective-permute-done.24
  151.6 4.8 %collective-permute-start.27 = (f32[3,2,1,512]{3,1,2,0:T(2,128)S(1)}, f32[3,2,1,512]{3,1,2,0:T(2,128)S(1)}, u32[]{:S(2)}, u32[]{:S(2)}) collective-permute-start(f32[3,2,1,512]{3,1,2,0:T(2,128)S(1)} %copy.226), channel_id=1, source_target_pairs={{0,8},{8,16},{16,24},{1,9},{9,17},{17,25},{2,10},{10,18},{18,26},{... | collective-permute-start | bytes 36872 | tf_op jit(solution)/shard_map/ppermute | solution.py:34
  156.6 5.9 %collective-permute-start.26 = (f32[3,2,64,1]{3,2,1,0:T(8,128)S(1)}, f32[3,2,64,1]{3,2,1,0:T(8,128)S(1)}, u32[]{:S(2)}, u32[]{:S(2)}) collective-permute-start(f32[3,2,64,1]{3,2,1,0:T(8,128)S(1)} %pad_maximum_fusion.47), channel_id=1, source_target_pairs={{0,1},{1,2},{2,3},{3,4},{4,5},{5,6},{6,7},{8,9},{9,10},{10,11},{11... | collective-permute-start | bytes 4616 | tf_op jit(solution)/shard_map/ppermute | solution.py:34
  167.4 3.8 collective-permute-done.28
  172.2 4.8 %collective-permute-start.31 = (f32[3,2,1,512]{3,1,2,0:T(2,128)S(1)}, f32[3,2,1,512]{3,1,2,0:T(2,128)S(1)}, u32[]{:S(2)}, u32[]{:S(2)}) collective-permute-start(f32[3,2,1,512]{3,1,2,0:T(2,128)S(1)} %copy.235), channel_id=1, source_target_pairs={{0,8},{8,16},{16,24},{1,9},{9,17},{17,25},{2,10},{10,18},{18,26},{... | collective-permute-start | bytes 36872 | tf_op jit(solution)/shard_map/ppermute | solution.py:34
  177.1 5.9 %collective-permute-start.30 = (f32[3,2,64,1]{3,2,1,0:T(8,128)S(1)}, f32[3,2,64,1]{3,2,1,0:T(8,128)S(1)}, u32[]{:S(2)}, u32[]{:S(2)}) collective-permute-start(f32[3,2,64,1]{3,2,1,0:T(8,128)S(1)} %slice.1123), channel_id=1, source_target_pairs={{0,1},{1,2},{2,3},{3,4},{4,5},{5,6},{6,7},{8,9},{9,10},{10,11},{11... | collective-permute-start | bytes 4616 | tf_op jit(solution)/shard_map/ppermute | solution.py:34
  187.3 4.3 all-to-all-start.1
  192.0 14.2 %all-to-all-done.1 = f32[2,4,64,512]{3,2,0,1:T(8,128)S(1)} async-done(((f32[2,4,64,512]{3,2,0,1:T(8,128)}), f32[2,4,64,512]{3,2,0,1:T(8,128)S(1)}, u32[]{:S(2)}, u32[]{:S(2)}) %all-to-all-start.1) | async-done | bytes 1048608 | tf_op jit(solution)/shard_map/all_to_all | solution.py:169
  206.3 1.3 copy.241
  207.6 1.3 select_select_fusion
  209.7 1.4 collective-permute-start.33
  211.1 4.5 %collective-permute-start.32 = (f32[3,1,512]{2,1,0:T(1,128)S(1)}, f32[3,1,512]{2,1,0:T(1,128)S(1)}, u32[]{:S(2)}, u32[]{:S(2)}) collective-permute-start(f32[3,1,512]{2,1,0:T(1,128)S(1)} %copy.243), channel_id=1, source_target_pairs={{0,8},{8,16},{16,24},{1,9},{9,17},{17,25},{2,10},{10,18},{18,26},{... | collective-permute-start | bytes 18440 | tf_op jit(solution)/shard_map/ppermute | solution.py:25
  219.4 5.6 %collective-permute-start.37 = (f32[1,512]{0,1:T(8,128)}, f32[1,512]{0,1:T(8,128)}, u32[]{:S(2)}, u32[]{:S(2)}) collective-permute-start(f32[1,512]{0,1:T(8,128)} %copy.253), channel_id=1, source_target_pairs={{0,8},{8,16},{16,24},{1,9},{9,17},{17,25},{2,10},{10,18},{18,26},{... | collective-permute-start | bytes 6152 | tf_op jit(solution)/shard_map/ppermute | solution.py:25
  227.7 1.4 collective-permute-start.35
  229.2 3.0 collective-permute-start.34
  234.3 5.2 %collective-permute-start.39 = (f32[258,1]{0,1:T(1,128)S(1)}, f32[258,1]{0,1:T(1,128)S(1)}, u32[]{:S(2)}, u32[]{:S(2)}) collective-permute-start(f32[258,1]{0,1:T(1,128)S(1)} %get-tuple-element.110), channel_id=1, source_target_pairs={{0,1},{1,2},{2,3},{3,4},{4,5},{5,6},{6,7},{8,9},{9,10},{10,11},{11... | collective-permute-start | bytes 3104 | tf_op jit(solution)/shard_map/ppermute | solution.py:25
  240.4 3.3 fusion.160
  243.8 3.9 collective-permute-start.41
  249.1 4.7 %collective-permute-done.41 = f32[1,512]{0,1:T(8,128)S(1)} collective-permute-done((f32[1,512]{0,1:T(8,128)S(1)}, f32[1,512]{0,1:T(8,128)S(1)}, u32[]{:S(2)}, u32[]{:S(2)}) %collective-permute-start.41) | collective-permute-done | bytes 2080 | tf_op jit(solution)/shard_map/ppermute | solution.py:25
  253.8 6.3 %collective-permute-done.40 = f32[1,512]{0,1:T(8,128)S(1)} collective-permute-done((f32[1,512]{0,1:T(8,128)S(1)}, f32[1,512]{0,1:T(8,128)S(1)}, u32[]{:S(2)}, u32[]{:S(2)}) %collective-permute-start.40) | collective-permute-done | bytes 2080 | tf_op jit(solution)/shard_map/ppermute | solution.py:26
  261.4 3.1 collective-permute-start.43
  265.3 1.4 multiply_reduce_fusion.3
  266.7 42.6 %all-reduce.18 = (f32[]{:T(128)}, f32[]{:T(128)}) all-reduce(f32[]{:T(128)} %get-tuple-element.20, f32[]{:T(128)} %get-tuple-element.19), channel_id=1, replica_groups=mesh['grp'=4,'tile'=8] {'grp','tile'}, use_global_device_ids=true, to_apply=%region_2.3 | all-reduce | flops 2 | bytes 16 | tf_op jit(solution)/shard_map/psum | solution.py:126
  311.0 4.3 collective-permute-start.45
  316.6 2.6 collective-permute-done.45
  319.2 7.3 %collective-permute-done.44 = f32[1,512]{0,1:T(8,128)S(1)} collective-permute-done((f32[1,512]{0,1:T(8,128)S(1)}, f32[1,512]{0,1:T(8,128)S(1)}, u32[]{:S(2)}, u32[]{:S(2)}) %collective-permute-start.44) | collective-permute-done | bytes 2080 | tf_op jit(solution)/shard_map/ppermute | solution.py:26
  327.8 3.0 collective-permute-start.47
  331.7 2.1 multiply_reduce_fusion.1
  333.8 40.1 %all-reduce.17 = (f32[]{:T(128)}, f32[]{:T(128)}) all-reduce(f32[]{:T(128)} %get-tuple-element.18, f32[]{:T(128)} %get-tuple-element.17), channel_id=1, replica_groups=mesh['grp'=4,'tile'=8] {'grp','tile'}, use_global_device_ids=true, to_apply=%region_6.7 | all-reduce | flops 2 | bytes 16 | tf_op jit(solution)/shard_map/psum | solution.py:126
  378.5 1.3 fusion.157
  380.0 4.3 collective-permute-start.49
  385.6 4.1 collective-permute-done.49
  389.7 7.5 %collective-permute-done.48 = f32[1,512]{0,1:T(8,128)S(1)} collective-permute-done((f32[1,512]{0,1:T(8,128)S(1)}, f32[1,512]{0,1:T(8,128)S(1)}, u32[]{:S(2)}, u32[]{:S(2)}) %collective-permute-start.48) | collective-permute-done | bytes 2080 | tf_op jit(solution)/shard_map/ppermute | solution.py:26
  398.7 3.0 collective-permute-start.51
  402.6 1.3 fusion.8
  403.9 40.4 %all-reduce.16 = (f32[]{:T(128)}, f32[]{:T(128)}) all-reduce(f32[]{:T(128)} %get-tuple-element.16, f32[]{:T(128)} %get-tuple-element.15), channel_id=1, replica_groups=mesh['grp'=4,'tile'=8] {'grp','tile'}, use_global_device_ids=true, to_apply=%region_10.11 | all-reduce | flops 2 | bytes 16 | tf_op jit(solution)/shard_map/psum | solution.py:126
  (282 shorter events, 68.7 us)
Async XLA Ops:
  1.5 13.7 %collective-permute-start = (f32[2,2,1,512]{3,1,2,0:T(2,128)S(1)}, f32[2,2,1,512]{3,1,2,0:T(2,128)S(1)}, u32[]{:S(2)}, u32[]{:S(2)}) collective-permute-start(f32[2,2,1,512]{3,1,2,0:T(2,128)S(1)} %copy.263), channel_id=1, source_target_pairs={{8,0},{16,8},{24,16},{9,1},{17,9},{25,17},{10,2},{18,10},{26,18},{... | collective-permute-start | bytes 24584 | tf_op jit(solution)/shard_map/ppermute | solution.py:34
  3.7 11.5 %collective-permute-start.1 = (f32[2,2,64,1]{3,2,1,0:T(8,128)S(1)}, f32[2,2,64,1]{3,2,1,0:T(8,128)S(1)}, u32[]{:S(2)}, u32[]{:S(2)}) collective-permute-start(f32[2,2,64,1]{3,2,1,0:T(8,128)S(1)} %slice.750), channel_id=1, source_target_pairs={{1,0},{2,1},{3,2},{4,3},{5,4},{6,5},{7,6},{9,8},{10,9},{11,10},{12... | collective-permute-start | bytes 3080 | tf_op jit(solution)/shard_map/ppermute | solution.py:34
  8.3 33.9 %all-to-all-start = ((f32[2,2,4,64,512]{4,3,0,1,2:T(8,128)}), f32[2,2,4,64,512]{4,3,0,1,2:T(8,128)}, u32[]{:S(2)}, u32[]{:S(2)}) async-start(f32[2,2,4,64,512]{4,3,0,1,2:T(8,128)} %copy.184), calls=%async_computation | async-start | bytes 4194304 | tf_op jit(solution)/shard_map/all_to_all | solution.py:152
  17.2 21.6 %collective-permute-start.3 = (f32[3,2,1,512]{3,1,2,0:T(2,128)S(1)}, f32[3,2,1,512]{3,1,2,0:T(2,128)S(1)}, u32[]{:S(2)}, u32[]{:S(2)}) collective-permute-start(f32[3,2,1,512]{3,1,2,0:T(2,128)S(1)} %copy.182), channel_id=1, source_target_pairs={{0,8},{8,16},{16,24},{1,9},{9,17},{17,25},{2,10},{10,18},{18,26},{... | collective-permute-start | bytes 36872 | tf_op jit(solution)/shard_map/ppermute | solution.py:34
  21.2 17.5 %collective-permute-start.2 = (f32[3,2,64,1]{3,2,1,0:T(8,128)S(1)}, f32[3,2,64,1]{3,2,1,0:T(8,128)S(1)}, u32[]{:S(2)}, u32[]{:S(2)}) collective-permute-start(f32[3,2,64,1]{3,2,1,0:T(8,128)S(1)} %pad_maximum_fusion.53), channel_id=1, source_target_pairs={{0,1},{1,2},{2,3},{3,4},{4,5},{5,6},{6,7},{8,9},{9,10},{10,11},{11... | collective-permute-start | bytes 4616 | tf_op jit(solution)/shard_map/ppermute | solution.py:34
  45.5 5.5 %collective-permute-start.4 = (f32[2,2,1,512]{3,1,2,0:T(2,128)S(1)}, f32[2,2,1,512]{3,1,2,0:T(2,128)S(1)}, u32[]{:S(2)}, u32[]{:S(2)}) collective-permute-start(f32[2,2,1,512]{3,1,2,0:T(2,128)S(1)} %copy.189), channel_id=1, source_target_pairs={{8,0},{16,8},{24,16},{9,1},{17,9},{25,17},{10,2},{18,10},{26,18},{... | collective-permute-start | bytes 24584 | tf_op jit(solution)/shard_map/ppermute | solution.py:34
  46.8 4.2 collective-permute-start.5
  51.9 8.8 %collective-permute-start.7 = (f32[3,2,1,512]{3,1,2,0:T(2,128)S(1)}, f32[3,2,1,512]{3,1,2,0:T(2,128)S(1)}, u32[]{:S(2)}, u32[]{:S(2)}) collective-permute-start(f32[3,2,1,512]{3,1,2,0:T(2,128)S(1)} %copy.191), channel_id=1, source_target_pairs={{0,8},{8,16},{16,24},{1,9},{9,17},{17,25},{2,10},{10,18},{18,26},{... | collective-permute-start | bytes 36872 | tf_op jit(solution)/shard_map/ppermute | solution.py:34
  55.9 5.9 %collective-permute-start.6 = (f32[3,2,64,1]{3,2,1,0:T(8,128)S(1)}, f32[3,2,64,1]{3,2,1,0:T(8,128)S(1)}, u32[]{:S(2)}, u32[]{:S(2)}) collective-permute-start(f32[3,2,64,1]{3,2,1,0:T(8,128)S(1)} %pad_maximum_fusion.52), channel_id=1, source_target_pairs={{0,1},{1,2},{2,3},{3,4},{4,5},{5,6},{6,7},{8,9},{9,10},{10,11},{11... | collective-permute-start | bytes 4616 | tf_op jit(solution)/shard_map/ppermute | solution.py:34
  63.0 6.0 %collective-permute-start.8 = (f32[2,2,1,512]{3,1,2,0:T(2,128)S(1)}, f32[2,2,1,512]{3,1,2,0:T(2,128)S(1)}, u32[]{:S(2)}, u32[]{:S(2)}) collective-permute-start(f32[2,2,1,512]{3,1,2,0:T(2,128)S(1)} %copy.196), channel_id=1, source_target_pairs={{8,0},{16,8},{24,16},{9,1},{17,9},{25,17},{10,2},{18,10},{26,18},{... | collective-permute-start | bytes 24584 | tf_op jit(solution)/shard_map/ppermute | solution.py:34
  64.3 4.7 %collective-permute-start.9 = (f32[2,2,64,1]{3,2,1,0:T(8,128)S(1)}, f32[2,2,64,1]{3,2,1,0:T(8,128)S(1)}, u32[]{:S(2)}, u32[]{:S(2)}) collective-permute-start(f32[2,2,64,1]{3,2,1,0:T(8,128)S(1)} %slice.1014), channel_id=1, source_target_pairs={{1,0},{2,1},{3,2},{4,3},{5,4},{6,5},{7,6},{9,8},{10,9},{11,10},{12... | collective-permute-start | bytes 3080 | tf_op jit(solution)/shard_map/ppermute | solution.py:34
  69.9 10.8 %collective-permute-start.11 = (f32[3,2,1,512]{3,1,2,0:T(2,128)S(1)}, f32[3,2,1,512]{3,1,2,0:T(2,128)S(1)}, u32[]{:S(2)}, u32[]{:S(2)}) collective-permute-start(f32[3,2,1,512]{3,1,2,0:T(2,128)S(1)} %copy.198), channel_id=1, source_target_pairs={{0,8},{8,16},{16,24},{1,9},{9,17},{17,25},{2,10},{10,18},{18,26},{... | collective-permute-start | bytes 36872 | tf_op jit(solution)/shard_map/ppermute | solution.py:34
  74.8 6.9 %collective-permute-start.10 = (f32[3,2,64,1]{3,2,1,0:T(8,128)S(1)}, f32[3,2,64,1]{3,2,1,0:T(8,128)S(1)}, u32[]{:S(2)}, u32[]{:S(2)}) collective-permute-start(f32[3,2,64,1]{3,2,1,0:T(8,128)S(1)} %pad_maximum_fusion.51), channel_id=1, source_target_pairs={{0,1},{1,2},{2,3},{3,4},{4,5},{5,6},{6,7},{8,9},{9,10},{10,11},{11... | collective-permute-start | bytes 4616 | tf_op jit(solution)/shard_map/ppermute | solution.py:34
  83.0 6.4 %collective-permute-start.12 = (f32[2,2,1,512]{3,1,2,0:T(2,128)S(1)}, f32[2,2,1,512]{3,1,2,0:T(2,128)S(1)}, u32[]{:S(2)}, u32[]{:S(2)}) collective-permute-start(f32[2,2,1,512]{3,1,2,0:T(2,128)S(1)} %copy.203), channel_id=1, source_target_pairs={{8,0},{16,8},{24,16},{9,1},{17,9},{25,17},{10,2},{18,10},{26,18},{... | collective-permute-start | bytes 24584 | tf_op jit(solution)/shard_map/ppermute | solution.py:34
  84.3 5.1 %collective-permute-start.13 = (f32[2,2,64,1]{3,2,1,0:T(8,128)S(1)}, f32[2,2,64,1]{3,2,1,0:T(8,128)S(1)}, u32[]{:S(2)}, u32[]{:S(2)}) collective-permute-start(f32[2,2,64,1]{3,2,1,0:T(8,128)S(1)} %slice.1034), channel_id=1, source_target_pairs={{1,0},{2,1},{3,2},{4,3},{5,4},{6,5},{7,6},{9,8},{10,9},{11,10},{12... | collective-permute-start | bytes 3080 | tf_op jit(solution)/shard_map/ppermute | solution.py:34
  90.3 10.8 %collective-permute-start.15 = (f32[3,2,1,512]{3,1,2,0:T(2,128)S(1)}, f32[3,2,1,512]{3,1,2,0:T(2,128)S(1)}, u32[]{:S(2)}, u32[]{:S(2)}) collective-permute-start(f32[3,2,1,512]{3,1,2,0:T(2,128)S(1)} %copy.205), channel_id=1, source_target_pairs={{0,8},{8,16},{16,24},{1,9},{9,17},{17,25},{2,10},{10,18},{18,26},{... | collective-permute-start | bytes 36872 | tf_op jit(solution)/shard_map/ppermute | solution.py:34
  95.3 6.9 %collective-permute-start.14 = (f32[3,2,64,1]{3,2,1,0:T(8,128)S(1)}, f32[3,2,64,1]{3,2,1,0:T(8,128)S(1)}, u32[]{:S(2)}, u32[]{:S(2)}) collective-permute-start(f32[3,2,64,1]{3,2,1,0:T(8,128)S(1)} %pad_maximum_fusion.50), channel_id=1, source_target_pairs={{0,1},{1,2},{2,3},{3,4},{4,5},{5,6},{6,7},{8,9},{9,10},{10,11},{11... | collective-permute-start | bytes 4616 | tf_op jit(solution)/shard_map/ppermute | solution.py:34
  103.5 6.4 %collective-permute-start.16 = (f32[2,2,1,512]{3,1,2,0:T(2,128)S(1)}, f32[2,2,1,512]{3,1,2,0:T(2,128)S(1)}, u32[]{:S(2)}, u32[]{:S(2)}) collective-permute-start(f32[2,2,1,512]{3,1,2,0:T(2,128)S(1)} %copy.210), channel_id=1, source_target_pairs={{8,0},{16,8},{24,16},{9,1},{17,9},{25,17},{10,2},{18,10},{26,18},{... | collective-permute-start | bytes 24584 | tf_op jit(solution)/shard_map/ppermute | solution.py:34
  104.8 5.1 %collective-permute-start.17 = (f32[2,2,64,1]{3,2,1,0:T(8,128)S(1)}, f32[2,2,64,1]{3,2,1,0:T(8,128)S(1)}, u32[]{:S(2)}, u32[]{:S(2)}) collective-permute-start(f32[2,2,64,1]{3,2,1,0:T(8,128)S(1)} %slice.1054), channel_id=1, source_target_pairs={{1,0},{2,1},{3,2},{4,3},{5,4},{6,5},{7,6},{9,8},{10,9},{11,10},{12... | collective-permute-start | bytes 3080 | tf_op jit(solution)/shard_map/ppermute | solution.py:34
  110.8 10.8 %collective-permute-start.19 = (f32[3,2,1,512]{3,1,2,0:T(2,128)S(1)}, f32[3,2,1,512]{3,1,2,0:T(2,128)S(1)}, u32[]{:S(2)}, u32[]{:S(2)}) collective-permute-start(f32[3,2,1,512]{3,1,2,0:T(2,128)S(1)} %copy.212), channel_id=1, source_target_pairs={{0,8},{8,16},{16,24},{1,9},{9,17},{17,25},{2,10},{10,18},{18,26},{... | collective-permute-start | bytes 36872 | tf_op jit(solution)/shard_map/ppermute | solution.py:34
  115.7 6.9 %collective-permute-start.18 = (f32[3,2,64,1]{3,2,1,0:T(8,128)S(1)}, f32[3,2,64,1]{3,2,1,0:T(8,128)S(1)}, u32[]{:S(2)}, u32[]{:S(2)}) collective-permute-start(f32[3,2,64,1]{3,2,1,0:T(8,128)S(1)} %pad_maximum_fusion.49), channel_id=1, source_target_pairs={{0,1},{1,2},{2,3},{3,4},{4,5},{5,6},{6,7},{8,9},{9,10},{10,11},{11... | collective-permute-start | bytes 4616 | tf_op jit(solution)/shard_map/ppermute | solution.py:34
  123.9 6.4 %collective-permute-start.20 = (f32[2,2,1,512]{3,1,2,0:T(2,128)S(1)}, f32[2,2,1,512]{3,1,2,0:T(2,128)S(1)}, u32[]{:S(2)}, u32[]{:S(2)}) collective-permute-start(f32[2,2,1,512]{3,1,2,0:T(2,128)S(1)} %copy.217), channel_id=1, source_target_pairs={{8,0},{16,8},{24,16},{9,1},{17,9},{25,17},{10,2},{18,10},{26,18},{... | collective-permute-start | bytes 24584 | tf_op jit(solution)/shard_map/ppermute | solution.py:34
  125.2 5.1 %collective-permute-start.21 = (f32[2,2,64,1]{3,2,1,0:T(8,128)S(1)}, f32[2,2,64,1]{3,2,1,0:T(8,128)S(1)}, u32[]{:S(2)}, u32[]{:S(2)}) collective-permute-start(f32[2,2,64,1]{3,2,1,0:T(8,128)S(1)} %slice.1074), channel_id=1, source_target_pairs={{1,0},{2,1},{3,2},{4,3},{5,4},{6,5},{7,6},{9,8},{10,9},{11,10},{12... | collective-permute-start | bytes 3080 | tf_op jit(solution)/shard_map/ppermute | solution.py:34
  131.2 10.8 %collective-permute-start.23 = (f32[3,2,1,512]{3,1,2,0:T(2,128)S(1)}, f32[3,2,1,512]{3,1,2,0:T(2,128)S(1)}, u32[]{:S(2)}, u32[]{:S(2)}) collective-permute-start(f32[3,2,1,512]{3,1,2,0:T(2,128)S(1)} %copy.219), channel_id=1, source_target_pairs={{0,8},{8,16},{16,24},{1,9},{9,17},{17,25},{2,10},{10,18},{18,26},{... | collective-permute-start | bytes 36872 | tf_op jit(solution)/shard_map/ppermute | solution.py:34
  136.1 6.9 %collective-permute-start.22 = (f32[3,2,64,1]{3,2,1,0:T(8,128)S(1)}, f32[3,2,64,1]{3,2,1,0:T(8,128)S(1)}, u32[]{:S(2)}, u32[]{:S(2)}) collective-permute-start(f32[3,2,64,1]{3,2,1,0:T(8,128)S(1)} %pad_maximum_fusion.48), channel_id=1, source_target_pairs={{0,1},{1,2},{2,3},{3,4},{4,5},{5,6},{6,7},{8,9},{9,10},{10,11},{11... | collective-permute-start | bytes 4616 | tf_op jit(solution)/shard_map/ppermute | solution.py:34
  144.3 6.4 %collective-permute-start.24 = (f32[2,2,1,512]{3,1,2,0:T(2,128)S(1)}, f32[2,2,1,512]{3,1,2,0:T(2,128)S(1)}, u32[]{:S(2)}, u32[]{:S(2)}) collective-permute-start(f32[2,2,1,512]{3,1,2,0:T(2,128)S(1)} %copy.224), channel_id=1, source_target_pairs={{8,0},{16,8},{24,16},{9,1},{17,9},{25,17},{10,2},{18,10},{26,18},{... | collective-permute-start | bytes 24584 | tf_op jit(solution)/shard_map/ppermute | solution.py:34
  145.7 5.1 %collective-permute-start.25 = (f32[2,2,64,1]{3,2,1,0:T(8,128)S(1)}, f32[2,2,64,1]{3,2,1,0:T(8,128)S(1)}, u32[]{:S(2)}, u32[]{:S(2)}) collective-permute-start(f32[2,2,64,1]{3,2,1,0:T(8,128)S(1)} %slice.1094), channel_id=1, source_target_pairs={{1,0},{2,1},{3,2},{4,3},{5,4},{6,5},{7,6},{9,8},{10,9},{11,10},{12... | collective-permute-start | bytes 3080 | tf_op jit(solution)/shard_map/ppermute | solution.py:34
  151.6 10.8 %collective-permute-start.27 = (f32[3,2,1,512]{3,1,2,0:T(2,128)S(1)}, f32[3,2,1,512]{3,1,2,0:T(2,128)S(1)}, u32[]{:S(2)}, u32[]{:S(2)}) collective-permute-start(f32[3,2,1,512]{3,1,2,0:T(2,128)S(1)} %copy.226), channel_id=1, source_target_pairs={{0,8},{8,16},{16,24},{1,9},{9,17},{17,25},{2,10},{10,18},{18,26},{... | collective-permute-start | bytes 36872 | tf_op jit(solution)/shard_map/ppermute | solution.py:34
  156.6 6.9 %collective-permute-start.26 = (f32[3,2,64,1]{3,2,1,0:T(8,128)S(1)}, f32[3,2,64,1]{3,2,1,0:T(8,128)S(1)}, u32[]{:S(2)}, u32[]{:S(2)}) collective-permute-start(f32[3,2,64,1]{3,2,1,0:T(8,128)S(1)} %pad_maximum_fusion.47), channel_id=1, source_target_pairs={{0,1},{1,2},{2,3},{3,4},{4,5},{5,6},{6,7},{8,9},{9,10},{10,11},{11... | collective-permute-start | bytes 4616 | tf_op jit(solution)/shard_map/ppermute | solution.py:34
  164.8 6.4 %collective-permute-start.28 = (f32[2,2,1,512]{3,1,2,0:T(2,128)S(1)}, f32[2,2,1,512]{3,1,2,0:T(2,128)S(1)}, u32[]{:S(2)}, u32[]{:S(2)}) collective-permute-start(f32[2,2,1,512]{3,1,2,0:T(2,128)S(1)} %copy.232), channel_id=1, source_target_pairs={{8,0},{16,8},{24,16},{9,1},{17,9},{25,17},{10,2},{18,10},{26,18},{... | collective-permute-start | bytes 24584 | tf_op jit(solution)/shard_map/ppermute | solution.py:34
  166.1 5.1 %collective-permute-start.29 = (f32[2,2,64,1]{3,2,0,1:T(8,128)S(1)}, f32[2,2,64,1]{3,2,0,1:T(8,128)S(1)}, u32[]{:S(2)}, u32[]{:S(2)}) collective-permute-start(f32[2,2,64,1]{3,2,0,1:T(8,128)S(1)} %slice.1114), channel_id=1, source_target_pairs={{1,0},{2,1},{3,2},{4,3},{5,4},{6,5},{7,6},{9,8},{10,9},{11,10},{12... | collective-permute-start | bytes 3080 | tf_op jit(solution)/shard_map/ppermute | solution.py:34
  172.2 10.9 %collective-permute-start.31 = (f32[3,2,1,512]{3,1,2,0:T(2,128)S(1)}, f32[3,2,1,512]{3,1,2,0:T(2,128)S(1)}, u32[]{:S(2)}, u32[]{:S(2)}) collective-permute-start(f32[3,2,1,512]{3,1,2,0:T(2,128)S(1)} %copy.235), channel_id=1, source_target_pairs={{0,8},{8,16},{16,24},{1,9},{9,17},{17,25},{2,10},{10,18},{18,26},{... | collective-permute-start | bytes 36872 | tf_op jit(solution)/shard_map/ppermute | solution.py:34
  177.1 6.9 %collective-permute-start.30 = (f32[3,2,64,1]{3,2,1,0:T(8,128)S(1)}, f32[3,2,64,1]{3,2,1,0:T(8,128)S(1)}, u32[]{:S(2)}, u32[]{:S(2)}) collective-permute-start(f32[3,2,64,1]{3,2,1,0:T(8,128)S(1)} %slice.1123), channel_id=1, source_target_pairs={{0,1},{1,2},{2,3},{3,4},{4,5},{5,6},{6,7},{8,9},{9,10},{10,11},{11... | collective-permute-start | bytes 4616 | tf_op jit(solution)/shard_map/ppermute | solution.py:34
  187.3 18.9 %all-to-all-start.1 = ((f32[2,4,64,512]{3,2,0,1:T(8,128)}), f32[2,4,64,512]{3,2,0,1:T(8,128)S(1)}, u32[]{:S(2)}, u32[]{:S(2)}) async-start(f32[2,4,64,512]{3,2,0,1:T(8,128)} %pad_maximum_fusion.1), calls=%async_computation.1 | async-start | bytes 2097152 | tf_op jit(solution)/shard_map/all_to_all | solution.py:169
  209.7 17.6 %collective-permute-start.33 = (f32[3,1,512]{2,1,0:T(1,128)S(1)}, f32[3,1,512]{2,1,0:T(1,128)S(1)}, u32[]{:S(2)}, u32[]{:S(2)}) collective-permute-start(f32[3,1,512]{2,1,0:T(1,128)S(1)} %copy.245), channel_id=1, source_target_pairs={{8,0},{16,8},{24,16},{9,1},{17,9},{25,17},{10,2},{18,10},{26,18},{... | collective-permute-start | bytes 18440 | tf_op jit(solution)/shard_map/ppermute | solution.py:26
  211.1 15.9 %collective-permute-start.32 = (f32[3,1,512]{2,1,0:T(1,128)S(1)}, f32[3,1,512]{2,1,0:T(1,128)S(1)}, u32[]{:S(2)}, u32[]{:S(2)}) collective-permute-start(f32[3,1,512]{2,1,0:T(1,128)S(1)} %copy.243), channel_id=1, source_target_pairs={{0,8},{8,16},{16,24},{1,9},{9,17},{17,25},{2,10},{10,18},{18,26},{... | collective-permute-start | bytes 18440 | tf_op jit(solution)/shard_map/ppermute | solution.py:25
  217.3 14.9 %collective-permute-start.36 = (f32[1,512]{0,1:T(8,128)}, f32[1,512]{0,1:T(8,128)S(1)}, u32[]{:S(2)}, u32[]{:S(2)}) collective-permute-start(f32[1,512]{0,1:T(8,128)} %copy.250), channel_id=1, source_target_pairs={{8,0},{16,8},{24,16},{9,1},{17,9},{25,17},{10,2},{18,10},{26,18},{... | collective-permute-start | bytes 6152 | tf_op jit(solution)/shard_map/ppermute | solution.py:26
  219.4 12.8 %collective-permute-start.37 = (f32[1,512]{0,1:T(8,128)}, f32[1,512]{0,1:T(8,128)}, u32[]{:S(2)}, u32[]{:S(2)}) collective-permute-start(f32[1,512]{0,1:T(8,128)} %copy.253), channel_id=1, source_target_pairs={{0,8},{8,16},{16,24},{1,9},{9,17},{17,25},{2,10},{10,18},{18,26},{... | collective-permute-start | bytes 6152 | tf_op jit(solution)/shard_map/ppermute | solution.py:25
  227.7 11.8 %collective-permute-start.35 = (f32[3,258,1]{1,2,0:T(1,128)S(1)}, f32[3,258,1]{1,2,0:T(1,128)S(1)}, u32[]{:S(2)}, u32[]{:S(2)}) collective-permute-start(f32[3,258,1]{1,2,0:T(1,128)S(1)} %get-tuple-element.57), channel_id=1, source_target_pairs={{1,0},{2,1},{3,2},{4,3},{5,4},{6,5},{7,6},{9,8},{10,9},{11,10},{12... | collective-permute-start | bytes 9296 | tf_op jit(solution)/shard_map/ppermute | solution.py:26
  229.2 10.4 %collective-permute-start.34 = (f32[3,258,1]{1,2,0:T(1,128)S(1)}, f32[3,258,1]{1,2,0:T(1,128)S(1)}, u32[]{:S(2)}, u32[]{:S(2)}) collective-permute-start(f32[3,258,1]{1,2,0:T(1,128)S(1)} %get-tuple-element.58), channel_id=1, source_target_pairs={{0,1},{1,2},{2,3},{3,4},{4,5},{5,6},{6,7},{8,9},{9,10},{10,11},{11... | collective-permute-start | bytes 9296 | tf_op jit(solution)/shard_map/ppermute | solution.py:25
  233.0 6.9 %collective-permute-start.38 = (f32[258,1]{0,1:T(1,128)S(1)}, f32[258,1]{0,1:T(1,128)S(1)}, u32[]{:S(2)}, u32[]{:S(2)}) collective-permute-start(f32[258,1]{0,1:T(1,128)S(1)} %get-tuple-element.109), channel_id=1, source_target_pairs={{1,0},{2,1},{3,2},{4,3},{5,4},{6,5},{7,6},{9,8},{10,9},{11,10},{12... | collective-permute-start | bytes 3104 | tf_op jit(solution)/shard_map/ppermute | solution.py:26
  234.3 6.0 %collective-permute-start.39 = (f32[258,1]{0,1:T(1,128)S(1)}, f32[258,1]{0,1:T(1,128)S(1)}, u32[]{:S(2)}, u32[]{:S(2)}) collective-permute-start(f32[258,1]{0,1:T(1,128)S(1)} %get-tuple-element.110), channel_id=1, source_target_pairs={{0,1},{1,2},{2,3},{3,4},{4,5},{5,6},{6,7},{8,9},{9,10},{10,11},{11... | collective-permute-start | bytes 3104 | tf_op jit(solution)/shard_map/ppermute | solution.py:25
  243.7 23.0 %copy-start.4 = (f32[256,512]{0,1:T(8,128)}, f32[256,512]{0,1:T(8,128)S(1)}, u32[]{:S(2)}) copy-start(f32[256,512]{0,1:T(8,128)S(1)} %get-tuple-element.34) | copy-start | bytes 1572868
  243.7 23.0 %copy-start.6 = (f32[256,512]{0,1:T(8,128)}, f32[256,512]{0,1:T(8,128)S(1)}, u32[]{:S(2)}) copy-start(f32[256,512]{0,1:T(8,128)S(1)} %get-tuple-element.35) | copy-start | bytes 1572868
  243.7 23.0 %copy-start.9 = (f32[256,512]{0,1:T(8,128)}, f32[256,512]{0,1:T(8,128)S(1)}, u32[]{:S(2)}) copy-start(f32[256,512]{0,1:T(8,128)S(1)} %get-tuple-element.36) | copy-start | bytes 1572868
  243.7 23.0 %copy-start.12 = (f32[256,512]{0,1:T(8,128)}, f32[256,512]{0,1:T(8,128)S(1)}, u32[]{:S(2)}) copy-start(f32[256,512]{0,1:T(8,128)S(1)} %get-tuple-element.37) | copy-start | bytes 1572868
  243.8 9.9 %collective-permute-start.41 = (f32[1,512]{0,1:T(8,128)S(1)}, f32[1,512]{0,1:T(8,128)S(1)}, u32[]{:S(2)}, u32[]{:S(2)}) collective-permute-start(f32[1,512]{0,1:T(8,128)S(1)} %get-tuple-element.131), channel_id=1, source_target_pairs={{0,8},{8,16},{16,24},{1,9},{9,17},{17,25},{2,10},{10,18},{18,26},{... | collective-permute-start | bytes 6152 | tf_op jit(solution)/shard_map/ppermute | solution.py:25
  247.8 12.3 %collective-permute-start.40 = (f32[1,512]{0,1:T(8,128)S(1)}, f32[1,512]{0,1:T(8,128)S(1)}, u32[]{:S(2)}, u32[]{:S(2)}) collective-permute-start(f32[1,512]{0,1:T(8,128)S(1)} %get-tuple-element.132), channel_id=1, source_target_pairs={{8,0},{16,8},{24,16},{9,1},{17,9},{25,17},{10,2},{18,10},{26,18},{... | collective-permute-start | bytes 6152 | tf_op jit(solution)/shard_map/ppermute | solution.py:26
  260.1 4.4 collective-permute-start.42
  261.4 3.9 collective-permute-start.43
  265.3 45.4 %copy-start.15 = (f32[256,512]{0,1:T(8,128)S(1)}, f32[256,512]{0,1:T(8,128)}, u32[]{:S(2)}) copy-start(f32[256,512]{0,1:T(8,128)} %get-tuple-element.33) | copy-start | bytes 1572868
  311.0 8.2 %collective-permute-start.45 = (f32[1,512]{0,1:T(8,128)S(1)}, f32[1,512]{0,1:T(8,128)S(1)}, u32[]{:S(2)}, u32[]{:S(2)}) collective-permute-start(f32[1,512]{0,1:T(8,128)S(1)} %get-tuple-element.129), channel_id=1, source_target_pairs={{0,8},{8,16},{16,24},{1,9},{9,17},{17,25},{2,10},{10,18},{18,26},{... | collective-permute-start | bytes 6152 | tf_op jit(solution)/shard_map/ppermute | solution.py:25
  315.3 11.2 %collective-permute-start.44 = (f32[1,512]{0,1:T(8,128)S(1)}, f32[1,512]{0,1:T(8,128)S(1)}, u32[]{:S(2)}, u32[]{:S(2)}) collective-permute-start(f32[1,512]{0,1:T(8,128)S(1)} %get-tuple-element.130), channel_id=1, source_target_pairs={{8,0},{16,8},{24,16},{9,1},{17,9},{25,17},{10,2},{18,10},{26,18},{... | collective-permute-start | bytes 6152 | tf_op jit(solution)/shard_map/ppermute | solution.py:26
  326.5 4.3 collective-permute-start.46
  327.8 3.8 collective-permute-start.47
  379.8 21.9 %copy-start.17 = (f32[2,2,64,512]{3,2,0,1:T(8,128)S(1)}, f32[2,2,64,512]{3,2,0,1:T(8,128)}, u32[]{:S(2)}) copy-start(f32[2,2,64,512]{3,2,0,1:T(8,128)} %get-tuple-element.39) | copy-start | bytes 1572868
  380.0 22.6 %copy-start.8 = (f32[256,512]{0,1:T(8,128)S(1)}, f32[256,512]{0,1:T(8,128)}, u32[]{:S(2)}) copy-start(f32[256,512]{0,1:T(8,128)} %copy-done.6) | copy-start | bytes 1572868
  380.0 22.6 %copy-start.11 = (f32[256,512]{0,1:T(8,128)S(1)}, f32[256,512]{0,1:T(8,128)}, u32[]{:S(2)}) copy-start(f32[256,512]{0,1:T(8,128)} %copy-done.9) | copy-start | bytes 1572868
  380.0 22.6 %copy-start.14 = (f32[256,512]{0,1:T(8,128)S(1)}, f32[256,512]{0,1:T(8,128)}, u32[]{:S(2)}) copy-start(f32[256,512]{0,1:T(8,128)} %copy-done.12) | copy-start | bytes 1572868
  380.0 9.7 %collective-permute-start.49 = (f32[1,512]{0,1:T(8,128)S(1)}, f32[1,512]{0,1:T(8,128)S(1)}, u32[]{:S(2)}, u32[]{:S(2)}) collective-permute-start(f32[1,512]{0,1:T(8,128)S(1)} %get-tuple-element.127), channel_id=1, source_target_pairs={{0,8},{8,16},{16,24},{1,9},{9,17},{17,25},{2,10},{10,18},{18,26},{... | collective-permute-start | bytes 6152 | tf_op jit(solution)/shard_map/ppermute | solution.py:25
  384.3 12.9 %collective-permute-start.48 = (f32[1,512]{0,1:T(8,128)S(1)}, f32[1,512]{0,1:T(8,128)S(1)}, u32[]{:S(2)}, u32[]{:S(2)}) collective-permute-start(f32[1,512]{0,1:T(8,128)S(1)} %get-tuple-element.128), channel_id=1, source_target_pairs={{8,0},{16,8},{24,16},{9,1},{17,9},{25,17},{10,2},{18,10},{26,18},{... | collective-permute-start | bytes 6152 | tf_op jit(solution)/shard_map/ppermute | solution.py:26
  397.4 5.2 %collective-permute-start.50 = (f32[258,1]{0,1:T(1,128)S(1)}, f32[258,1]{0,1:T(1,128)S(1)}, u32[]{:S(2)}, u32[]{:S(2)}) collective-permute-start(f32[258,1]{0,1:T(1,128)S(1)} %get-tuple-element.101), channel_id=1, source_target_pairs={{1,0},{2,1},{3,2},{4,3},{5,4},{6,5},{7,6},{9,8},{10,9},{11,10},{12... | collective-permute-start | bytes 3104 | tf_op jit(solution)/shard_map/ppermute | solution.py:26
  398.7 3.9 collective-permute-start.51
  402.6 45.7 %copy-start.3 = (f32[256,512]{0,1:T(8,128)S(1)}, f32[256,512]{0,1:T(8,128)}, u32[]{:S(2)}) copy-start(f32[256,512]{0,1:T(8,128)} %copy.259) | copy-start | bytes 1572868
  (18 other events, 180.7 us)
where the time goes:
time: 452 us; the launch traced here: 449 us
  starting transfers between devices  164 us (36%)
  blocking collectives  123 us (27%)
  waiting for transfers between devices  97.7 us (22%)
  other arithmetic  36.8 us (8%)
  local copies, waits for them, and re-layouts  15.4 us (3%)
  between operations  12.4 us (3%)
    psum x3, blocking collectives, pair_sums(): lax.psum((jnp.sum(residual * precond), jnp.sum(precond * applied)), ('grp...  123 us
    ppermute x32, starting transfers between devices, passed_along(): return lax.ppermute(array, axis, pairs)  99.9 us
    ppermute x32, waiting for transfers between devices, passed_along(): return lax.ppermute(array, axis, pairs)  47.3 us
    ppermute x10, starting transfers between devices, extended(): before = lax.ppermute(last, axis, up)  40.1 us
    ppermute x10, waiting for transfers between devices, extended(): after = lax.ppermute(first, axis, down)  21.2 us
    all_to_all x1, waiting for transfers between devices, shards(): lax.all_to_all(parcel, 'grp', split_axis=1, concat_axis=1, tiled=True)  14.2 us
    ppermute x10, waiting for transfers between devices, extended(): before = lax.ppermute(last, axis, up)  13.3 us
    ppermute x10, starting transfers between devices, extended(): after = lax.ppermute(first, axis, down)  13.1 us
  transfers between devices with their start and end apart: 54, of which 26 were waited for; matrix products, arithmetic and copies ran while one was open for 4% of the time, Pallas kernels for 0%

commit v1 on v0

v1 whole, which is shorter than its diff:
```python
import functools

import jax
import jax.numpy as jnp
from jax import lax
from jax.experimental import pallas as pl
from jax.experimental.pallas import tpu as pltpu
from jax.sharding import PartitionSpec as P

BS = 8
NSUB = 8

DAMP = 0.05
RELAX = 0.2
STRENGTH = 0.5
DRAG = 1.0
STEP = 0.5

MESH = pl.DeviceIdType.MESH
F32 = jnp.float32
T = 8
L = 128
W = 12
TOP = 2 * T


def lanes(rows, width):
    return lax.broadcasted_iota(jnp.int32, (rows, width), 1)


def right(x):
    return pltpu.roll(x, x.shape[1] - 1, 1)


def left(x):
    return pltpu.roll(x, 1, 1)


def rows_of(shape):
    return lax.broadcasted_iota(jnp.int32, shape, 0)


def above(prev, here):
    return pltpu.roll(jnp.where(rows_of(here.shape) == T - 1, prev, here), 1, 0)


def below(here, after):
    return pltpu.roll(jnp.where(rows_of(here.shape) == 0, after, here), T - 1, 0)


def kernel(
    groups,
    tiles,
    base_in,
    depth_in,
    ssh_in,
    cur_in,
    land_ref,
    thick_in,
    ice_ref,
    vel_in,
    stress_in,
    wind_in,
    ssh_out,
    vel_out,
    stress_out,
    vel,
    st,
    wind,
    flow,
    h,
    kk,
    pp,
    qq,
    g,
    x,
    b,
    gd,
    v0,
    v1,
    v2,
    w0,
    w1,
    w2,
    wet,
    cover,
    pack_s,
    pack_r,
    opack_s,
    opack_r,
    sp,
    back,
    top_in,
    bot_in,
    red_s,
    red_r,
    red2_s,
    red2_r,
    load_sem,
    flow_send,
    flow_recv,
    row_send,
    row_recv,
    col_send,
    col_recv,
    back_send,
    back_recv,
    edge_send,
    edge_recv,
    red_send,
    red_recv,
    red2_send,
    red2_recv,
    out_sem,
):
    gi = lax.axis_index("grp")
    ti = lax.axis_index("tile")
    rows, cols = thick_in.shape[1], thick_in.shape[2]
    orows = base_in.shape[0]
    wide = cols + L
    end = TOP + rows
    oend = TOP + orows

    loads = []

    def load(src, dst):
        copy = pltpu.make_async_copy(src, dst, load_sem.at[len(loads)])
        copy.start()
        loads.append(copy)
        return copy

    load_thick = load(thick_in, h.at[:, TOP:end, 0:cols])
    load_depth = load(depth_in, g.at[TOP:oend, 0:cols])
    load_x = load(ssh_in, x.at[TOP:oend, 0:cols])
    load_b = load(base_in, b.at[TOP:oend, 0:cols])
    load_vel = load(vel_in, vel.at[:, :, TOP:end, 0:cols])
    load_st = load(stress_in, st.at[:, :, TOP:end, 0:cols])
    load_wind = load(wind_in, wind.at[:, :, TOP:end, 0:cols])

    def clear(ref, top, last, total):
        ref[..., 0:top, :] = jnp.zeros(ref.shape[:-2] + (top, wide), F32)
        ref[..., last:total, :] = jnp.zeros(ref.shape[:-2] + (total - last, wide), F32)
        ref[..., top:last, cols:wide] = jnp.zeros(ref.shape[:-2] + (last - top, L), F32)

    for ref in (vel, st, wind, flow, h):
        clear(ref, TOP, end, end + TOP)
    for ref in (g, x, b):
        clear(ref, TOP, oend, oend + TOP)
    for ref in (pack_r, opack_r):
        ref[...] = jnp.zeros_like(ref)

    barrier = pltpu.get_barrier_semaphore()
    for d in range(1, groups):
        pl.semaphore_signal(
            barrier, inc=1, device_id=(lax.rem(gi + d, groups), ti), device_id_type=MESH
        )
    for d in range(1, tiles):
        pl.semaphore_signal(
            barrier, inc=1, device_id=(gi, lax.rem(ti + d, tiles)), device_id_type=MESH
        )

    def blocks(ref, out, count):
        width = ref.shape[-1]
        row = lax.broadcasted_iota(jnp.int32, (width, cols), 0)
        spread = (row == lax.shift_right_logical(lanes(width, cols), 3)).astype(F32)
        values = ref[...].reshape((count, width)).astype(F32)
        out[...] = jnp.dot(values, spread, preferred_element_type=F32)

    blocks(land_ref, wet, land_ref.shape[0])
    for c in range(2):
        row = lax.broadcasted_iota(jnp.int32, (cols // BS, cols), 0)
        spread = (row == lax.shift_right_logical(lanes(cols // BS, cols), 3)).astype(F32)
        cover[c] = jnp.dot(ice_ref[c].astype(F32), spread, preferred_element_type=F32)

    pl.semaphore_wait(barrier, groups + tiles - 2)

    def flow_copy(cap, target):
        lo = max(0, rows * target - T)
        hi = min(rows * groups, rows * target + rows + T)
        start = TOP + lo - rows * target
        src = cur_in.at[:, lo:hi, :]
        dst = flow.at[:, cap, start : start + hi - lo, 0:cols]
        return src, dst

    homes = (0, groups - 1)
    for cap, home in enumerate(homes):

        @pl.when(gi == home)
        def _():
            order = sorted(range(groups), key=lambda k: -abs(k - home))
            for target in order:
                src, dst = flow_copy(cap, target)
                if target == home:
                    pltpu.make_async_copy(src, dst, flow_recv.at[cap]).start()
                else:
                    pltpu.make_async_remote_copy(
                        src_ref=src,
                        dst_ref=dst,
                        send_sem=flow_send.at[target],
                        recv_sem=flow_recv.at[cap],
                        device_id=(target, ti),
                        device_id_type=MESH,
                    ).start()

    def row_copies(which):
        out = []
        fields = (
            (vel_in, vel, rows, end),
            (stress_in, st, rows, end),
            (wind_in, wind, rows, end),
            (ssh_in, x, orows, oend),
            (base_in, b, orows, oend),
            (h, h, None, end),
            (g, g, None, oend),
        )
        for k, (src, dst, length, last) in enumerate(fields):
            if (k >= 5) != which:
                continue
            origin = TOP if length is None else 0
            span = (last - TOP) if length is None else length
            lead = (slice(None),) * (len(src.shape) - 2)
            for way in range(2):
                from_row = origin + span - T if way == 0 else origin
                to_row = TOP - T if way == 0 else last
                out.append(
                    (
                        way,
                        pltpu.make_async_remote_copy(
                            src_ref=src.at[lead + (slice(from_row, from_row + T), slice(0, cols))],
                            dst_ref=dst.at[lead + (slice(to_row, to_row + T), slice(0, cols))],
                            send_sem=row_send.at[2 * k + way],
                            recv_sem=row_recv.at[2 * k + way],
                            device_id=(
                                lax.rem(gi + (1 if way == 0 else groups - 1), groups),
                                ti,
                            ),
                            device_id_type=MESH,
                        ),
                    )
                )
        return out

    def edge(way, index, count):
        sends = index < count - 1 if way == 0 else index > 0
        receives = index > 0 if way == 0 else index < count - 1
        return sends, receives

    early = row_copies(False)
    for way, copy in early:
        pl.when(edge(way, gi, groups)[0])(copy.start)

    load_thick.wait()

    def cover_chunk(k, _):
        for c in range(2):
            at = (c, pl.ds(pl.multiple_of(TOP + k * T, T), T), pl.ds(0, cols))
            h[at] = h[at] * cover[c, pl.ds(k, 1), :]
        return 0

    lax.fori_loop(0, rows // T, cover_chunk, 0)
    load_depth.wait()

    def wet_chunk(k, _):
        at = (pl.ds(pl.multiple_of(TOP + k * T, T), T), pl.ds(0, cols))
        g[at] = g[at] * wet[pl.ds(k, 1), :]
        return 0

    lax.fori_loop(0, orows // T, wet_chunk, 0)
    late = row_copies(True)
    for way, copy in late:
        pl.when(edge(way, gi, groups)[0])(copy.start)
    load_vel.wait()
    load_st.wait()
    load_wind.wait()
    load_x.wait()
    load_b.wait()
    for way, copy in early + late:
        pl.when(edge(way, gi, groups)[1])(copy.wait_recv)

    lane = lanes(T, L)

    def col_copies(src, dst, base):
        out = []
        for way in range(2):
            out.append(
                (
                    way,
                    pltpu.make_async_remote_copy(
                        src_ref=src.at[way],
                        dst_ref=dst.at[way],
                        send_sem=col_send.at[base + way],
                        recv_sem=col_recv.at[base + way],
                        device_id=(gi, lax.rem(ti + (1 if way == 0 else tiles - 1), tiles)),
                        device_id_type=MESH,
                    ),
                )
            )
        return out

    def packed(values):
        after = jnp.zeros((T, L), F32)
        before = jnp.zeros((T, L), F32)
        for f, (first, last) in enumerate(values):
            here = (lane >= W * f) & (lane < W * f + W)
            after = jnp.where(here, pltpu.roll(last, (W * f + W) % L, 1), after)
            before = jnp.where(here, pltpu.roll(first, W * f, 1) if f else first, before)
        return after, before

    def unpacked(from_before, from_after, f):
        low = pltpu.roll(from_before, (L - W - W * f) % L, 1)
        high = pltpu.roll(from_after, (L - W * f) % L, 1) if f else from_after
        return jnp.where(lane < W, high, jnp.where(lane >= L - W, low, 0.0))

    ochunks = orows // T + 2
    ichunks = rows // T + 2

    def opack_chunk(k, _):
        at = pl.ds(pl.multiple_of(T + k * T, T), T)
        to = pl.ds(pl.multiple_of(k * T, T), T)
        after, before = packed(
            [(ref[at, pl.ds(0, L)], ref[at, pl.ds(cols - L, L)]) for ref in (g, x, b)]
        )
        opack_s[0, to, :] = after
        opack_s[1, to, :] = before
        return 0

    lax.fori_loop(0, ochunks, opack_chunk, 0)
    ocols = col_copies(opack_s, opack_r, 0)
    for way, copy in ocols:
        pl.when(edge(way, ti, tiles)[0])(copy.start)

    for target in range(groups):

        @pl.when(gi == target)
        def _():
            for cap, home in enumerate(homes):
                src, dst = flow_copy(cap, target)
                if target == home:
                    pltpu.make_async_copy(src, dst, flow_recv.at[cap]).wait()
                else:
                    pltpu.make_async_remote_copy(
                        src_ref=src,
                        dst_ref=dst,
                        send_sem=flow_send.at[target],
                        recv_sem=flow_recv.at[cap],
                        device_id=(home, ti),
                        device_id_type=MESH,
                    ).wait_recv()

    def ice_fields(c):
        return (
            vel.at[0, c],
            vel.at[1, c],
            st.at[0, c],
            st.at[1, c],
            st.at[2, c],
            h.at[c],
            wind.at[0, c],
            wind.at[1, c],
            flow.at[0, c],
            flow.at[1, c],
        )

    def pack_chunk(k, _):
        at = pl.ds(pl.multiple_of(T + k * T, T), T)
        to = pl.ds(pl.multiple_of(k * T, T), T)
        for c in range(2):
            after, before = packed(
                [(ref[at, pl.ds(0, L)], ref[at, pl.ds(cols - L, L)]) for ref in ice_fields(c)]
            )
            pack_s[0, c, to, :] = after
            pack_s[1, c, to, :] = before
        return 0

    lax.fori_loop(0, ichunks, pack_chunk, 0)
    icols = col_copies(pack_s, pack_r, 2)
    for way, copy in icols:
        pl.when(edge(way, ti, tiles)[0])(copy.start)

    for way, copy in ocols:
        pl.when(edge(way, ti, tiles)[1])(copy.wait_recv)

    def ounpack_chunk(k, _):
        at = pl.ds(pl.multiple_of(T + k * T, T), T)
        to = pl.ds(pl.multiple_of(k * T, T), T)
        for f, ref in enumerate((g, x, b)):
            ref[at, pl.ds(cols, L)] = unpacked(opack_r[0, to, :], opack_r[1, to, :], f)
        return 0

    lax.fori_loop(0, ochunks, ounpack_chunk, 0)

    for way, copy in icols:
        pl.when(edge(way, ti, tiles)[1])(copy.wait_recv)

    def unpack_chunk(k, _):
        at = pl.ds(pl.multiple_of(T + k * T, T), T)
        to = pl.ds(pl.multiple_of(k * T, T), T)
        for c in range(2):
            for f, ref in enumerate(ice_fields(c)):
                ref[at, pl.ds(cols, L)] = unpacked(pack_r[0, c, to, :], pack_r[1, c, to, :], f)
            thick = h[c, at, :]
            mass = thick + 1.0
            inverse = jnp.where(thick > 0.0, 1.0 / (mass + STEP * DRAG), 0.0)
            q = STEP * inverse
            kk[c, at, :] = (RELAX * STRENGTH / (1.0 + RELAX)) * thick
            pp[c, at, :] = mass * inverse
            qq[c, at, :] = q
            for comp in range(2):
                wind[comp, c, at, :] = q * (wind[comp, c, at, :] + DRAG * flow[comp, c, at, :])
        return 0

    lax.fori_loop(0, ichunks, unpack_chunk, 0)

    keep = 1.0 / (1.0 + RELAX)

    def ice_chunk(k, _):
        r = pl.multiple_of(T + k * T, T)
        at = pl.ds(r, T)
        up = pl.ds(pl.multiple_of(r - T, T), T)
        down = pl.ds(pl.multiple_of(r + T, T), T)
        for c in range(2):
            u = vel[0, c, at, :]
            v = vel[1, c, at, :]
            du_dx = below(u, vel[0, c, down, :]) - u
            dv_dx = below(v, vel[1, c, down, :]) - v
            du_dy = right(u) - u
            dv_dy = right(v) - v
            ed = du_dx + dv_dy
            et = du_dx - dv_dy
            es = du_dy + dv_dx
            inverse = lax.rsqrt(ed * ed + et * et + es * es + 1.0)
            k0 = kk[c, at, :]
            k1 = k0 * inverse
            s0 = st[0, c, at, :] * keep + (k1 * ed - k0)
            s1 = st[1, c, at, :] * keep + k1 * et
            s2 = st[2, c, at, :] * keep + k1 * es
            st[0, c, at, :] = s0
            st[1, c, at, :] = s1
            st[2, c, at, :] = s2
            total = s0 + s1
            diff = s0 - s1
            total_up = above(st[0, c, up, :] + st[1, c, up, :], total)
            s2_up = above(st[2, c, up, :], s2)
            fx = 0.5 * (total - total_up) + (s2 - left(s2))
            fy = 0.5 * (diff - left(diff)) + (s2 - s2_up)
            p = pp[c, at, :]
            q = qq[c, at, :]
            vel[0, c, at, :] = p * u + (q * fx + wind[0, c, at, :])
            vel[1, c, at, :] = p * v + (q * fy + wind[1, c, at, :])
        return 0

    def subcycle(n, _):
        return lax.fori_loop(0, ichunks, ice_chunk, 0)

    lax.fori_loop(0, NSUB, subcycle, 0)

    sub = lax.broadcasted_iota(jnp.int32, (T, wide), 0)

    def drag(comp, c, where):
        return jnp.where(
            h[c, where, :] > 0.0, DRAG * (vel[comp, c, where, :] - flow[comp, c, where, :]), 0.0
        )

    def drag_chunk(k, _):
        r = pl.multiple_of(TOP + k * T, T)
        to = pl.ds(pl.multiple_of(k * T, T), T)
        for c in range(2):
            d0 = drag(0, c, pl.ds(r, T))
            d0_up = above(drag(0, c, pl.ds(pl.multiple_of(r - T, T), T)), d0)
            d0_up = jnp.where((sub == 0) & (k == 0), 0.0, d0_up)
            d1 = drag(1, c, pl.ds(r, T))
            sp[c, to, :] = (d0 - d0_up) + (d1 - left(d1))
        return 0

    lax.fori_loop(0, rows // T, drag_chunk, 0)
    for c in range(2):
        sp[c, rows : rows + T, :] = drag(0, c, pl.ds(end - T, T))

    outs = [
        pltpu.make_async_copy(vel.at[:, :, TOP:end, 0:cols], vel_out, out_sem.at[0]),
        pltpu.make_async_copy(st.at[:, :, TOP:end, 0:cols], stress_out, out_sem.at[1]),
    ]

    def back_copy(cap, source, target):
        return pltpu.make_async_remote_copy(
            src_ref=sp.at[cap],
            dst_ref=back.at[source],
            send_sem=back_send.at[cap],
            recv_sem=back_recv.at[source],
            device_id=(target, ti),
            device_id_type=MESH,
        )

    def to_top():
        return pltpu.make_async_remote_copy(
            src_ref=sp.at[0, rows - T : rows + T, :],
            dst_ref=top_in,
            send_sem=edge_send.at[0],
            recv_sem=edge_recv.at[0],
            device_id=(1, ti),
            device_id_type=MESH,
        )

    def to_bot():
        return pltpu.make_async_remote_copy(
            src_ref=sp.at[1, 0:T, :],
            dst_ref=bot_in,
            send_sem=edge_send.at[1],
            recv_sem=edge_recv.at[1],
            device_id=(groups - 2, ti),
            device_id_type=MESH,
        )

    pl.when(gi == groups - 1)(lambda: to_top().start())
    pl.when(gi == 0)(lambda: to_bot().start())
    for cap, home in enumerate(homes):
        for source in range(groups):

            @pl.when(gi == source)
            def _():
                if source == home:
                    pltpu.make_async_copy(
                        sp.at[cap], back.at[source], back_recv.at[source]
                    ).start()
                else:
                    back_copy(cap, source, home).start()

    for copy in outs:
        copy.start()

    for cap, home in enumerate(homes):

        @pl.when(gi == home)
        def _():
            for source in range(groups):
                if source == home:
                    pltpu.make_async_copy(
                        sp.at[cap], back.at[source], back_recv.at[source]
                    ).wait()
                else:
                    back_copy(cap, source, source).wait_recv()
            for source in range(groups):

                def add_chunk(k, _):
                    at = pl.ds(pl.multiple_of(TOP + source * rows + k * T, T), T)
                    b[at, :] = b[at, :] + back[source, pl.ds(pl.multiple_of(k * T, T), T), :]
                    return 0

                lax.fori_loop(0, rows // T, add_chunk, 0)
            for source in range(groups):
                row = TOP + (source + 1) * rows
                b[row : row + 1, :] = (
                    b[row : row + 1, :] - back[source, rows + T - 1 : rows + T, :]
                )

    @pl.when(gi == 1)
    def _():
        to_top().wait_recv()
        b[T:TOP, :] = b[T:TOP, :] + top_in[0:T, :]
        b[TOP : TOP + 1, :] = b[TOP : TOP + 1, :] - top_in[2 * T - 1 : 2 * T, :]

    @pl.when(gi == groups - 2)
    def _():
        to_bot().wait_recv()
        b[oend : oend + T, :] = b[oend : oend + T, :] + bot_in[...]

    zero = jnp.zeros((T, L), F32)

    def fold(value):
        total = value[:, 0:L]
        for j in range(1, cols // L):
            total = total + value[:, j * L : (j + 1) * L]
        return total

    def owned(k):
        return jnp.where((k >= 1) & (k <= orows // T), 1.0, 0.0).astype(F32)

    def around(ref, r):
        middle = ref[pl.ds(r, T), :]
        up = above(ref[pl.ds(pl.multiple_of(r - T, T), T), :], middle)
        down = below(middle, ref[pl.ds(pl.multiple_of(r + T, T), T), :])
        return (up + down) + (left(middle) + right(middle))

    for ref in (w0, w1, w2):
        ref[0:T, :] = jnp.zeros((T, wide), F32)
        ref[oend + T :, :] = jnp.zeros((T, wide), F32)

    def first_chunk(k, sums):
        r = pl.multiple_of(T + k * T, T)
        at = pl.ds(r, T)
        up, down = pl.ds(pl.multiple_of(r - T, T), T), pl.ds(pl.multiple_of(r + T, T), T)
        g0, gu, gw = g[at, :], g[up, :], g[down, :]
        x_0 = x[at, :]
        gx = g0 * x_0
        g_near = (above(gu, g0) + below(g0, gw)) + (left(g0) + right(g0))
        diag = DAMP + g0 * g_near
        near = (above(gu * x[up, :], gx) + below(gx, gw * x[down, :])) + (left(gx) + right(gx))
        r0 = jnp.where(g0 > 0.0, b[at, :], 0.0) - diag * x_0 + g0 * near
        inverse = 1.0 / diag
        z = r0 * inverse
        v0[at, :] = z
        w0[at, :] = g0 * z
        gd[at, :] = g0 * inverse
        return sums + owned(k) * fold(r0 * z)

    m0 = lax.fori_loop(0, ochunks, first_chunk, zero)

    def power(w_from, v_to, w_to):
        def chunk(k, sums):
            r = pl.multiple_of(T + k * T, T)
            at = pl.ds(r, T)
            near = around(w_from, r)
            v = gd[at, :] * near
            w = g[at, :] * v
            v_to[at, :] = v
            w_to[at, :] = w
            own = owned(k)
            return (
                sums[0] + own * fold(w_from[at, :] * near),
                sums[1] + own * fold(w * near),
            )

        return lax.fori_loop(0, ochunks, chunk, (zero, zero))

    m1, m2 = power(w0, v1, w1)
    m3, m4 = power(w1, v2, w2)

    def last_chunk(k, sums):
        r = pl.multiple_of(TOP + k * T, T)
        return sums + fold(w2[pl.ds(r, T), :] * around(w2, r))

    m5 = lax.fori_loop(0, orows // T, last_chunk, zero)

    row = lax.broadcasted_iota(jnp.int32, (T, L), 0)
    moments = zero
    for k, m in enumerate((m0, m1, m2, m3, m4, m5)):
        moments = jnp.where(row == k, jnp.sum(m, axis=0, keepdims=True), moments)

    def all_reduce(value, src, dst, send, recv, index, count, device):
        src[...] = value
        for d in range(1, count):
            pltpu.make_async_remote_copy(
                src_ref=src,
                dst_ref=dst.at[d],
                send_sem=send.at[d],
                recv_sem=recv.at[d],
                device_id=device(lax.rem(index + d, count)),
                device_id_type=MESH,
            ).start()
        for d in range(1, count):
            copy = pltpu.make_async_remote_copy(
                src_ref=src,
                dst_ref=dst.at[d],
                send_sem=send.at[d],
                recv_sem=recv.at[d],
                device_id=device(lax.rem(index + d, count)),
                device_id_type=MESH,
            )
            copy.wait()
        for d in range(1, count):
            value = value + dst[d]
        return value

    moments = all_reduce(
        moments, red_s, red_r, red_send, red_recv, ti, tiles, lambda k: (gi, k)
    )
    moments = all_reduce(
        moments, red2_s, red2_r, red2_send, red2_recv, gi, groups, lambda k: (k, ti)
    )
    total = jnp.sum(moments, axis=1, keepdims=True)
    nu = [total[k : k + 1, :] for k in range(6)]
    a = [nu[k] - nu[k + 1] for k in range(5)]

    tiny = 1e-12

    def safe(value, scale):
        ok = value > tiny * scale
        return jnp.where(ok, 1.0 / jnp.where(ok, value, 1.0), 0.0)

    i0 = safe(a[0], 0.0 * a[0])
    l10, l20 = a[1] * i0, a[2] * i0
    d1 = a[2] - l10 * a[1]
    i1 = safe(d1, a[2])
    e21 = a[3] - l20 * a[1]
    l21 = e21 * i1
    d2 = a[4] - l20 * a[2] - l21 * e21
    i2 = safe(d2, a[4])
    y0 = nu[0]
    y1 = nu[1] - l10 * y0
    y2 = nu[2] - l20 * y0 - l21 * y1
    c2 = y2 * i2
    c1 = y1 * i1 - l21 * c2
    c0 = y0 * i0 - l10 * c1 - l20 * c2

    def final_chunk(k, _):
        at = (pl.ds(pl.multiple_of(TOP + k * T, T), T), pl.ds(0, cols))
        x[at] = x[at] + (c0 * v0[at] + (c1 * v1[at] + c2 * v2[at]))
        return 0

    lax.fori_loop(0, orows // T, final_chunk, 0)
    last = pltpu.make_async_copy(x.at[TOP:oend, 0:cols], ssh_out, out_sem.at[2])
    last.start()

    for way, copy in early + late:
        pl.when(edge(way, gi, groups)[0])(copy.wait_send)
    for way, copy in ocols + icols:
        pl.when(edge(way, ti, tiles)[0])(copy.wait_send)
    for cap, home in enumerate(homes):

        @pl.when(gi == home)
        def _():
            for target in range(groups):
                if target != home:
                    src, dst = flow_copy(cap, target)
                    pltpu.make_async_remote_copy(
                        src_ref=src,
                        dst_ref=dst,
                        send_sem=flow_send.at[target],
                        recv_sem=flow_recv.at[cap],
                        device_id=(target, ti),
                        device_id_type=MESH,
                    ).wait_send()

        @pl.when(gi != home)
        def _():
            back_copy(cap, 0, home).wait_send()

    pl.when(gi == groups - 1)(lambda: to_top().wait_send())
    pl.when(gi == 0)(lambda: to_bot().wait_send())
    for copy in outs:
        copy.wait()
    last.wait()


def step(groups, tiles, *args):
    base_rhs, thick, ice_vel, ice_stress = args[0], args[5], args[7], args[8]
    orows, cols = base_rhs.shape
    rows = thick.shape[1]
    irows = rows + 2 * TOP
    erows = orows + 2 * TOP
    wide = cols + L
    any_spec = pl.BlockSpec(memory_space=pl.ANY)
    vmem = pl.BlockSpec(memory_space=pltpu.VMEM)
    dma = pltpu.SemaphoreType.DMA
    ice = pltpu.VMEM((2, irows, wide), F32)
    ocean = pltpu.VMEM((erows, wide), F32)
    return pl.pallas_call(
        functools.partial(kernel, groups, tiles),
        out_shape=(
            jax.ShapeDtypeStruct(base_rhs.shape, F32),
            jax.ShapeDtypeStruct(ice_vel.shape, F32),
            jax.ShapeDtypeStruct(ice_stress.shape, F32),
        ),
        in_specs=[any_spec] * 4 + [vmem, any_spec, vmem] + [any_spec] * 3,
        out_specs=(any_spec,) * 3,
        scratch_shapes=[
            pltpu.VMEM((2, 2, irows, wide), F32),
            pltpu.VMEM((3, 2, irows, wide), F32),
            pltpu.VMEM((2, 2, irows, wide), F32),
            pltpu.VMEM((2, 2, irows, wide), F32),
            ice,
            ice,
            ice,
            ice,
        ]
        + [ocean] * 10
        + [
            pltpu.VMEM((orows // BS, cols), F32),
            pltpu.VMEM((2, rows // BS, cols), F32),
            pltpu.VMEM((2, 2, rows + 2 * T, L), F32),
            pltpu.VMEM((2, 2, rows + 2 * T, L), F32),
            pltpu.VMEM((2, orows + 2 * T, L), F32),
            pltpu.VMEM((2, orows + 2 * T, L), F32),
            pltpu.VMEM((2, rows + T, wide), F32),
            pltpu.VMEM((groups, rows + T, wide), F32),
            pltpu.VMEM((2 * T, wide), F32),
            pltpu.VMEM((T, wide), F32),
            pltpu.VMEM((T, L), F32),
            pltpu.VMEM((tiles, T, L), F32),
            pltpu.VMEM((T, L), F32),
            pltpu.VMEM((groups, T, L), F32),
            dma((7,)),
            dma((groups,)),
            dma((2,)),
            dma((14,)),
            dma((14,)),
            dma((4,)),
            dma((4,)),
            dma((2,)),
            dma((groups,)),
            dma((2,)),
            dma((2,)),
            dma((tiles,)),
            dma((tiles,)),
            dma((groups,)),
            dma((groups,)),
            dma((3,)),
        ],
        compiler_params=pltpu.CompilerParams(
            collective_id=0, has_side_effects=True, vmem_limit_bytes=48 * 1024 * 1024
        ),
    )(*args)


def solution(mesh):
    grid = P("grp", "tile")
    plane = P(None, "grp", "tile")
    stack = P(None, None, "grp", "tile")
    return jax.shard_map(
        functools.partial(step, mesh.shape["grp"], mesh.shape["tile"]),
        mesh=mesh,
        in_specs=(grid, grid, grid, plane, grid, plane, plane, stack, stack, stack),
        out_specs=(grid, stack, stack),
        check_vma=False,
    )
```

time: 452 us -> 99.9 us (0.22)
  starting transfers between devices: 164 us -> 0 us
  blocking collectives: 123 us -> 0 us
  waiting for transfers between devices: 97.7 us -> 0 us
  Pallas kernels: 0 us -> 87.6 us
  other arithmetic: 36.8 us -> 0 us
  between operations: 12.4 us -> 0.66 us
    ppermute x52 -> x0, starting transfers between devices: 153 us -> none  [the longest x32 99.9 us: passed_along(): return lax.ppermute(array, axis, pairs)]
    psum x3 -> x0, blocking collectives: 123 us -> none  [pair_sums(): lax.psum((jnp.sum(residual * precond), jnp.sum(precond * applied)), ('grp...]
    pallas_call x0 -> x1, Pallas kernels: none -> 87.6 us  [step(): pl.pallas_call(functools.partial(kernel, groups, tiles), out_shape=(jax.S...]
    ppermute x52 -> x0, waiting for transfers between devices: 81.8 us -> none  [the longest x32 47.3 us: passed_along(): return lax.ppermute(array, axis, pairs)]
    all_to_all x2 -> x0, waiting for transfers between devices: 16 us -> none  [the longest x1 14.2 us: shards(): lax.all_to_all(parcel, 'grp', split_axis=1, concat_axis=1, tiled=True)]
    all_to_all x2 -> x0, starting transfers between devices: 10.8 us -> none  [the longest x1 6.47 us: shards(): lax.all_to_all(outgoing, 'grp', split_axis=2, concat_axis=2, tiled=True)]
    div x10 -> x0, other arithmetic: 7.94 us -> none  [the longest x3 4.79 us: shards(): precond = residual / diagonal]
    mul x16 -> x0, other arithmetic: 7.23 us -> none  [the longest x7 2.22 us: relax_stress(): (previous[1] + RELAX * strength * tens_rate / deformation) * relax_scale]
  transfers between devices with their start and end apart: 54 -> 0, of which waited for: 26 -> 0; matrix products, arithmetic and copies ran while one was open for 4% -> 0% of each run, Pallas kernels for 0% -> 0%
where the time goes in v1:
time: 99.9 us; the launch traced here: 99.4 us
  Pallas kernels  87.6 us (88%)
  local copies, waits for them, and re-layouts  11.2 us (11%)
    pallas_call x1, Pallas kernels, step(): pl.pallas_call(functools.partial(kernel, groups, tiles), out_shape=(jax.S...  87.6 us
    unnamed x21, local copies, waits for them, and re-layouts  11.2 us

profile of v1, /device:TPU:0, one launch (start us, length us, event | category | flops | bytes accessed | tf_op | source)
XLA Modules:
  0.0 99.4 jit_solution(3319519448253918372)
XLA Ops:
  0.6 0.0 copy-start
  0.6 1.1 %copy-done = f32[3,2,64,512]{3,2,1,0:T(8,128)S(1)} copy-done((f32[3,2,64,512]{3,2,1,0:T(8,128)S(1)}, f32[3,2,64,512]{3,2,1,0:T(8,128)}, u32[]{:S(2)}) %copy-start) | copy-done | bytes 786456
  1.8 0.0 copy-start.1
  1.8 1.0 %copy-done.1 = f32[256,512]{1,0:T(8,128)S(1)} copy-done((f32[256,512]{1,0:T(8,128)S(1)}, f32[256,512]{1,0:T(8,128)}, u32[]{:S(2)}) %copy-start.1) | copy-done | bytes 524312
  2.8 0.0 copy-start.2
  2.8 1.0 %copy-done.2 = f32[256,512]{1,0:T(8,128)S(1)} copy-done((f32[256,512]{1,0:T(8,128)S(1)}, f32[256,512]{1,0:T(8,128)}, u32[]{:S(2)}) %copy-start.2) | copy-done | bytes 524312
  3.9 0.0 copy-start.3
  3.9 1.0 %copy-done.3 = f32[256,512]{1,0:T(8,128)S(1)} copy-done((f32[256,512]{1,0:T(8,128)S(1)}, f32[256,512]{1,0:T(8,128)}, u32[]{:S(2)}) %copy-start.3) | copy-done | bytes 524312
  4.9 0.0 copy-start.4
  4.9 1.0 %copy-done.4 = f32[2,2,64,512]{3,2,1,0:T(8,128)S(1)} copy-done((f32[2,2,64,512]{3,2,1,0:T(8,128)S(1)}, f32[2,2,64,512]{3,2,1,0:T(8,128)}, u32[]{:S(2)}) %copy-start.4) | copy-done | bytes 524312
  5.9 0.0 copy-start.5
  5.9 1.0 %copy-done.5 = f32[2,2,64,512]{3,2,1,0:T(8,128)S(1)} copy-done((f32[2,2,64,512]{3,2,1,0:T(8,128)S(1)}, f32[2,2,64,512]{3,2,1,0:T(8,128)}, u32[]{:S(2)}) %copy-start.5) | copy-done | bytes 524312
  7.0 0.0 copy-start.6
  7.0 0.9 copy-done.6
  7.9 0.0 copy-start.7
  7.9 0.7 copy-done.7
  8.6 0.0 copy-start.8
  8.6 0.7 copy-done.8
  9.3 87.6 %shard_map.121 = (f32[256,512]{1,0:T(8,128)S(1)}, f32[2,2,64,512]{3,2,1,0:T(8,128)S(1)}, f32[3,2,64,512]{3,2,1,0:T(8,128)S(1)}) custom-call(f32[256,512]{1,0:T(8,128)S(1)} %copy-done.1, f32[256,512]{1,0:T(8,128)S(1)} %copy-done.2, f32[256,512]{1,0:T(8,128)S(1)} %copy-done.3, f32[2,256,512]{2,1,0:T(8,128)} %cur_in.1, s32[32,64]{1,0:T(8,128)S(1)} %copy-done.7, ...), custom_call_target="tpu_custom_call" | custom-call | tf_op jit(solution)/shard_map/pallas_call | solution.py:747
  96.9 0.8 copy.16
  97.7 0.8 copy.17
  98.5 0.9 copy.18
Async XLA Ops:
  0.6 1.1 %copy-start = (f32[3,2,64,512]{3,2,1,0:T(8,128)S(1)}, f32[3,2,64,512]{3,2,1,0:T(8,128)}, u32[]{:S(2)}) copy-start(f32[3,2,64,512]{3,2,1,0:T(8,128)} %stress_in.1) | copy-start | bytes 2359300
  1.8 1.0 %copy-start.1 = (f32[256,512]{1,0:T(8,128)S(1)}, f32[256,512]{1,0:T(8,128)}, u32[]{:S(2)}) copy-start(f32[256,512]{1,0:T(8,128)} %base_in.1) | copy-start | bytes 1572868
  2.8 1.0 %copy-start.2 = (f32[256,512]{1,0:T(8,128)S(1)}, f32[256,512]{1,0:T(8,128)}, u32[]{:S(2)}) copy-start(f32[256,512]{1,0:T(8,128)} %depth_in.1) | copy-start | bytes 1572868
  3.9 1.0 %copy-start.3 = (f32[256,512]{1,0:T(8,128)S(1)}, f32[256,512]{1,0:T(8,128)}, u32[]{:S(2)}) copy-start(f32[256,512]{1,0:T(8,128)} %ssh_in.1) | copy-start | bytes 1572868
  4.9 1.0 %copy-start.4 = (f32[2,2,64,512]{3,2,1,0:T(8,128)S(1)}, f32[2,2,64,512]{3,2,1,0:T(8,128)}, u32[]{:S(2)}) copy-start(f32[2,2,64,512]{3,2,1,0:T(8,128)} %vel_in.1) | copy-start | bytes 1572868
  5.9 1.0 %copy-start.5 = (f32[2,2,64,512]{3,2,1,0:T(8,128)S(1)}, f32[2,2,64,512]{3,2,1,0:T(8,128)}, u32[]{:S(2)}) copy-start(f32[2,2,64,512]{3,2,1,0:T(8,128)} %wind_in.1) | copy-start | bytes 1572868
  7.0 0.9 copy-start.6
  7.9 0.7 copy-start.7
  8.6 0.7 copy-start.8

commit v2 on v1

--- a/solution.py
+++ b/solution.py
@@ -214,7 +214,7 @@
             (g, g, None, oend),
         )
         for k, (src, dst, length, last) in enumerate(fields):
-            if (k >= 5) != which:
+            if k not in which:
                 continue
             origin = TOP if length is None else 0
             span = (last - TOP) if length is None else length
@@ -245,7 +245,7 @@
         receives = index > 0 if way == 0 else index < count - 1
         return sends, receives
 
-    early = row_copies(False)
+    early = row_copies((0, 1, 2))
     for way, copy in early:
         pl.when(edge(way, gi, groups)[0])(copy.start)
 
@@ -258,6 +258,9 @@
         return 0
 
     lax.fori_loop(0, rows // T, cover_chunk, 0)
+    late = row_copies((5,))
+    for way, copy in late:
+        pl.when(edge(way, gi, groups)[0])(copy.start)
     load_depth.wait()
 
     def wet_chunk(k, _):
@@ -265,10 +268,7 @@
         g[at] = g[at] * wet[pl.ds(k, 1), :]
         return 0
 
-    lax.fori_loop(0, orows // T, wet_chunk, 0)
-    late = row_copies(True)
-    for way, copy in late:
-        pl.when(edge(way, gi, groups)[0])(copy.start)
+    lax.fori_loop(0, orows // T, wet_chunk, 0, unroll=4)
     load_vel.wait()
     load_st.wait()
     load_wind.wait()
@@ -314,21 +314,6 @@
     ochunks = orows // T + 2
     ichunks = rows // T + 2
 
-    def opack_chunk(k, _):
-        at = pl.ds(pl.multiple_of(T + k * T, T), T)
-        to = pl.ds(pl.multiple_of(k * T, T), T)
-        after, before = packed(
-            [(ref[at, pl.ds(0, L)], ref[at, pl.ds(cols - L, L)]) for ref in (g, x, b)]
-        )
-        opack_s[0, to, :] = after
-        opack_s[1, to, :] = before
-        return 0
-
-    lax.fori_loop(0, ochunks, opack_chunk, 0)
-    ocols = col_copies(opack_s, opack_r, 0)
-    for way, copy in ocols:
-        pl.when(edge(way, ti, tiles)[0])(copy.start)
-
     for target in range(groups):
 
         @pl.when(gi == target)
@@ -372,25 +357,17 @@
             pack_s[1, c, to, :] = before
         return 0
 
-    lax.fori_loop(0, ichunks, pack_chunk, 0)
+    lax.fori_loop(0, ichunks, pack_chunk, 0, unroll=2)
     icols = col_copies(pack_s, pack_r, 2)
     for way, copy in icols:
         pl.when(edge(way, ti, tiles)[0])(copy.start)
 
-    for way, copy in ocols:
-        pl.when(edge(way, ti, tiles)[1])(copy.wait_recv)
-
-    def ounpack_chunk(k, _):
-        at = pl.ds(pl.multiple_of(T + k * T, T), T)
-        to = pl.ds(pl.multiple_of(k * T, T), T)
-        for f, ref in enumerate((g, x, b)):
-            ref[at, pl.ds(cols, L)] = unpacked(opack_r[0, to, :], opack_r[1, to, :], f)
-        return 0
-
-    lax.fori_loop(0, ochunks, ounpack_chunk, 0)
-
     for way, copy in icols:
         pl.when(edge(way, ti, tiles)[1])(copy.wait_recv)
+
+    orow = row_copies((3, 4, 6))
+    for way, copy in orow:
+        pl.when(edge(way, gi, groups)[0])(copy.start)
 
     def unpack_chunk(k, _):
         at = pl.ds(pl.multiple_of(T + k * T, T), T)
@@ -409,7 +386,7 @@
                 wind[comp, c, at, :] = q * (wind[comp, c, at, :] + DRAG * flow[comp, c, at, :])
         return 0
 
-    lax.fori_loop(0, ichunks, unpack_chunk, 0)
+    lax.fori_loop(0, ichunks, unpack_chunk, 0, unroll=2)
 
     keep = 1.0 / (1.0 + RELAX)
 
@@ -450,9 +427,29 @@
         return 0
 
     def subcycle(n, _):
-        return lax.fori_loop(0, ichunks, ice_chunk, 0)
-
-    lax.fori_loop(0, NSUB, subcycle, 0)
+        return lax.fori_loop(0, ichunks, ice_chunk, 0, unroll=10)
+
+    lax.fori_loop(0, NSUB // 2, subcycle, 0)
+
+    for way, copy in orow:
+        pl.when(edge(way, gi, groups)[1])(copy.wait_recv)
+
+    def opack_chunk(k, _):
+        at = pl.ds(pl.multiple_of(T + k * T, T), T)
+        to = pl.ds(pl.multiple_of(k * T, T), T)
+        after, before = packed(
+            [(ref[at, pl.ds(0, L)], ref[at, pl.ds(cols - L, L)]) for ref in (g, x, b)]
+        )
+        opack_s[0, to, :] = after
+        opack_s[1, to, :] = before
+        return 0
+
+    lax.fori_loop(0, ochunks, opack_chunk, 0, unroll=2)
+    ocols = col_copies(opack_s, opack_r, 0)
+    for way, copy in ocols:
+        pl.when(edge(way, ti, tiles)[0])(copy.start)
+
+    lax.fori_loop(NSUB // 2, NSUB, subcycle, 0)
 
     sub = lax.broadcasted_iota(jnp.int32, (T, wide), 0)
 
@@ -472,7 +469,7 @@
             sp[c, to, :] = (d0 - d0_up) + (d1 - left(d1))
         return 0
 
-    lax.fori_loop(0, rows // T, drag_chunk, 0)
+    lax.fori_loop(0, rows // T, drag_chunk, 0, unroll=4)
     for c in range(2):
         sp[c, rows : rows + T, :] = drag(0, c, pl.ds(end - T, T))
 
@@ -527,6 +524,60 @@
 
     for copy in outs:
         copy.start()
+
+    for way, copy in ocols:
+        pl.when(edge(way, ti, tiles)[1])(copy.wait_recv)
+
+    def ounpack_chunk(k, _):
+        at = pl.ds(pl.multiple_of(T + k * T, T), T)
+        to = pl.ds(pl.multiple_of(k * T, T), T)
+        for f, ref in enumerate((g, x, b)):
+            ref[at, pl.ds(cols, L)] = unpacked(opack_r[0, to, :], opack_r[1, to, :], f)
+        return 0
+
+    lax.fori_loop(0, ochunks, ounpack_chunk, 0, unroll=2)
+
+    zero = jnp.zeros((T, L), F32)
+
+    def fold(value):
+        total = value[:, 0:L]
+        for j in range(1, cols // L):
+            total = total + value[:, j * L : (j + 1) * L]
+        return total
+
+    def owned(k):
+        return jnp.where((k >= 1) & (k <= orows // T), 1.0, 0.0).astype(F32)
+
+    def around(ref, r):
+        middle = ref[pl.ds(r, T), :]
+        up = above(ref[pl.ds(pl.multiple_of(r - T, T), T), :], middle)
+        down = below(middle, ref[pl.ds(pl.multiple_of(r + T, T), T), :])
+        return (up + down) + (left(middle) + right(middle))
+
+    for ref in (w0, w1, w2):
+        ref[0:T, :] = jnp.zeros((T, wide), F32)
+        ref[oend + T :, :] = jnp.zeros((T, wide), F32)
+
+    def pre_chunk(k, _):
+        r = pl.multiple_of(T + k * T, T)
+        at = pl.ds(r, T)
+        up, down = pl.ds(pl.multiple_of(r - T, T), T), pl.ds(pl.multiple_of(r + T, T), T)
+        g0, gu, gw = g[at, :], g[up, :], g[down, :]
+        x_0 = x[at, :]
+        gx = g0 * x_0
+        g_near = (above(gu, g0) + below(g0, gw)) + (left(g0) + right(g0))
+        diag = DAMP + g0 * g_near
+        near = (above(gu * x[up, :], gx) + below(gx, gw * x[down, :])) + (left(gx) + right(gx))
+        b[at, :] = jnp.where(g0 > 0.0, b[at, :], 0.0) - diag * x_0 + g0 * near
+        inverse = 1.0 / diag
+        v2[at, :] = inverse
+        gd[at, :] = g0 * inverse
+        return 0
+
+    lax.fori_loop(0, ochunks, pre_chunk, 0, unroll=2)
+
+    def add(at, value):
+        b[at, :] = b[at, :] + jnp.where(g[at, :] > 0.0, value, 0.0)
 
     for cap, home in enumerate(homes):
 
@@ -543,67 +594,34 @@
 
                 def add_chunk(k, _):
                     at = pl.ds(pl.multiple_of(TOP + source * rows + k * T, T), T)
-                    b[at, :] = b[at, :] + back[source, pl.ds(pl.multiple_of(k * T, T), T), :]
+                    add(at, back[source, pl.ds(pl.multiple_of(k * T, T), T), :])
                     return 0
 
-                lax.fori_loop(0, rows // T, add_chunk, 0)
+                lax.fori_loop(0, rows // T, add_chunk, 0, unroll=4)
             for source in range(groups):
                 row = TOP + (source + 1) * rows
-                b[row : row + 1, :] = (
-                    b[row : row + 1, :] - back[source, rows + T - 1 : rows + T, :]
-                )
+                add(slice(row, row + 1), -back[source, rows + T - 1 : rows + T, :])
 
     @pl.when(gi == 1)
     def _():
         to_top().wait_recv()
-        b[T:TOP, :] = b[T:TOP, :] + top_in[0:T, :]
-        b[TOP : TOP + 1, :] = b[TOP : TOP + 1, :] - top_in[2 * T - 1 : 2 * T, :]
+        add(slice(T, TOP), top_in[0:T, :])
+        add(slice(TOP, TOP + 1), -top_in[2 * T - 1 : 2 * T, :])
 
     @pl.when(gi == groups - 2)
     def _():
         to_bot().wait_recv()
-        b[oend : oend + T, :] = b[oend : oend + T, :] + bot_in[...]
-
-    zero = jnp.zeros((T, L), F32)
-
-    def fold(value):
-        total = value[:, 0:L]
-        for j in range(1, cols // L):
-            total = total + value[:, j * L : (j + 1) * L]
-        return total
-
-    def owned(k):
-        return jnp.where((k >= 1) & (k <= orows // T), 1.0, 0.0).astype(F32)
-
-    def around(ref, r):
-        middle = ref[pl.ds(r, T), :]
-        up = above(ref[pl.ds(pl.multiple_of(r - T, T), T), :], middle)
-        down = below(middle, ref[pl.ds(pl.multiple_of(r + T, T), T), :])
-        return (up + down) + (left(middle) + right(middle))
-
-    for ref in (w0, w1, w2):
-        ref[0:T, :] = jnp.zeros((T, wide), F32)
-        ref[oend + T :, :] = jnp.zeros((T, wide), F32)
+        add(slice(oend, oend + T), bot_in[...])
 
     def first_chunk(k, sums):
-        r = pl.multiple_of(T + k * T, T)
-        at = pl.ds(r, T)
-        up, down = pl.ds(pl.multiple_of(r - T, T), T), pl.ds(pl.multiple_of(r + T, T), T)
-        g0, gu, gw = g[at, :], g[up, :], g[down, :]
-        x_0 = x[at, :]
-        gx = g0 * x_0
-        g_near = (above(gu, g0) + below(g0, gw)) + (left(g0) + right(g0))
-        diag = DAMP + g0 * g_near
-        near = (above(gu * x[up, :], gx) + below(gx, gw * x[down, :])) + (left(gx) + right(gx))
-        r0 = jnp.where(g0 > 0.0, b[at, :], 0.0) - diag * x_0 + g0 * near
-        inverse = 1.0 / diag
-        z = r0 * inverse
+        at = pl.ds(pl.multiple_of(T + k * T, T), T)
+        r0 = b[at, :]
+        z = r0 * v2[at, :]
         v0[at, :] = z
-        w0[at, :] = g0 * z
-        gd[at, :] = g0 * inverse
+        w0[at, :] = g[at, :] * z
         return sums + owned(k) * fold(r0 * z)
 
-    m0 = lax.fori_loop(0, ochunks, first_chunk, zero)
+    m0 = lax.fori_loop(0, ochunks, first_chunk, zero, unroll=2)
 
     def power(w_from, v_to, w_to):
         def chunk(k, sums):
@@ -620,7 +638,7 @@
                 sums[1] + own * fold(w * near),
             )
 
-        return lax.fori_loop(0, ochunks, chunk, (zero, zero))
+        return lax.fori_loop(0, ochunks, chunk, (zero, zero), unroll=2)
 
     m1, m2 = power(w0, v1, w1)
     m3, m4 = power(w1, v2, w2)
@@ -629,7 +647,7 @@
         r = pl.multiple_of(TOP + k * T, T)
         return sums + fold(w2[pl.ds(r, T), :] * around(w2, r))
 
-    m5 = lax.fori_loop(0, orows // T, last_chunk, zero)
+    m5 = lax.fori_loop(0, orows // T, last_chunk, zero, unroll=2)
 
     row = lax.broadcasted_iota(jnp.int32, (T, L), 0)
     moments = zero
@@ -697,11 +715,11 @@
         x[at] = x[at] + (c0 * v0[at] + (c1 * v1[at] + c2 * v2[at]))
         return 0
 
-    lax.fori_loop(0, orows // T, final_chunk, 0)
+    lax.fori_loop(0, orows // T, final_chunk, 0, unroll=4)
     last = pltpu.make_async_copy(x.at[TOP:oend, 0:cols], ssh_out, out_sem.at[2])
     last.start()
 
-    for way, copy in early + late:
+    for way, copy in early + late + orow:
         pl.when(edge(way, gi, groups)[0])(copy.wait_send)
     for way, copy in ocols + icols:
         pl.when(edge(way, ti, tiles)[0])(copy.wait_send)
@@ -740,6 +758,7 @@
     erows = orows + 2 * TOP
     wide = cols + L
     any_spec = pl.BlockSpec(memory_space=pl.ANY)
+    hbm = pl.BlockSpec(memory_space=pltpu.HBM)
     vmem = pl.BlockSpec(memory_space=pltpu.VMEM)
     dma = pltpu.SemaphoreType.DMA
     ice = pltpu.VMEM((2, irows, wide), F32)
@@ -751,7 +770,7 @@
             jax.ShapeDtypeStruct(ice_vel.shape, F32),
             jax.ShapeDtypeStruct(ice_stress.shape, F32),
         ),
-        in_specs=[any_spec] * 4 + [vmem, any_spec, vmem] + [any_spec] * 3,
+        in_specs=[hbm] * 4 + [vmem, hbm, vmem] + [hbm] * 3,
         out_specs=(any_spec,) * 3,
         scratch_shapes=[
             pltpu.VMEM((2, 2, irows, wide), F32),
@@ -797,7 +816,7 @@
             dma((3,)),
         ],
         compiler_params=pltpu.CompilerParams(
-            collective_id=0, has_side_effects=True, vmem_limit_bytes=48 * 1024 * 1024
+            collective_id=0, has_side_effects=True, vmem_limit_bytes=67_043_328
         ),
     )(*args)
 

time: 99.9 us -> 72.5 us (0.73)
  Pallas kernels: 87.6 us -> 66.9 us
  local copies, waits for them, and re-layouts: 11.2 us -> 4.69 us
    pallas_call x1, Pallas kernels: 87.6 us -> 66.9 us  [step(): pl.pallas_call(functools.partial(kernel, groups, tiles), out_shape=(jax.S...]
    unnamed x21 -> x5, local copies, waits for them, and re-layouts: 11.2 us -> 4.69 us
where the time goes in v2:
time: 72.5 us; the launch traced here: 72.2 us
  Pallas kernels  66.9 us (92%)
  local copies, waits for them, and re-layouts  4.69 us (6%)
    pallas_call x1, Pallas kernels, step(): pl.pallas_call(functools.partial(kernel, groups, tiles), out_shape=(jax.S...  66.9 us
    unnamed x5, local copies, waits for them, and re-layouts  4.69 us

profile of v2, /device:TPU:0, one launch (start us, length us, event | category | flops | bytes accessed | tf_op | source)
XLA Modules:
  0.0 72.2 jit_solution(3459116422350048478)
XLA Ops:
  0.6 66.9 %shard_map.121 = (f32[256,512]{1,0:T(8,128)}, f32[2,2,64,512]{3,2,1,0:T(8,128)}, f32[3,2,64,512]{3,2,1,0:T(8,128)}) custom-call(f32[256,512]{1,0:T(8,128)} %base_in.1, f32[256,512]{1,0:T(8,128)} %depth_in.1, f32[256,512]{1,0:T(8,128)} %ssh_in.1, f32[2,256,512]{2,1,0:T(8,128)} %cur_in.1, s32[32,64]{1,0:T(8,128)} %land_ref.1, f32[2,64,512]{2,1,0:T(8,128)} %thick_in.1, ...), custom_call_target="tpu_custom_call" | custom-call | tf_op jit(solution)/shard_map/pallas_call | solution.py:766
  67.5 0.0 copy-start
  67.5 1.9 %copy.16 = f32[256,512]{1,0:T(8,128)} copy(f32[256,512]{1,0:T(8,128)} %get-tuple-element.6) | data formatting | bytes 1048576
  69.5 1.9 %copy.17 = f32[2,2,64,512]{3,2,1,0:T(8,128)} copy(f32[2,2,64,512]{3,2,1,0:T(8,128)} %get-tuple-element.7) | data formatting | bytes 1048576
  71.4 0.0 copy-done
  71.4 0.9 %copy.18 = f32[3,2,64,512]{3,2,1,0:T(8,128)} copy(f32[3,2,64,512]{3,2,1,0:T(8,128)S(1)} %copy-done) | data formatting | bytes 1572864
Async XLA Ops:
  67.5 3.8 %copy-start = (f32[3,2,64,512]{3,2,1,0:T(8,128)S(1)}, f32[3,2,64,512]{3,2,1,0:T(8,128)}, u32[]{:S(2)}) copy-start(f32[3,2,64,512]{3,2,1,0:T(8,128)} %get-tuple-element.8) | copy-start | bytes 2359300

commit v3 on v2

--- a/solution.py
+++ b/solution.py
@@ -357,7 +357,7 @@
             pack_s[1, c, to, :] = before
         return 0
 
-    lax.fori_loop(0, ichunks, pack_chunk, 0, unroll=2)
+    lax.fori_loop(0, ichunks, pack_chunk, 0, unroll=5)
     icols = col_copies(pack_s, pack_r, 2)
     for way, copy in icols:
         pl.when(edge(way, ti, tiles)[0])(copy.start)
@@ -386,7 +386,7 @@
                 wind[comp, c, at, :] = q * (wind[comp, c, at, :] + DRAG * flow[comp, c, at, :])
         return 0
 
-    lax.fori_loop(0, ichunks, unpack_chunk, 0, unroll=2)
+    lax.fori_loop(0, ichunks, unpack_chunk, 0, unroll=5)
 
     keep = 1.0 / (1.0 + RELAX)
 
@@ -444,7 +444,7 @@
         opack_s[1, to, :] = before
         return 0
 
-    lax.fori_loop(0, ochunks, opack_chunk, 0, unroll=2)
+    lax.fori_loop(0, ochunks, opack_chunk, 0, unroll=17)
     ocols = col_copies(opack_s, opack_r, 0)
     for way, copy in ocols:
         pl.when(edge(way, ti, tiles)[0])(copy.start)
@@ -535,7 +535,7 @@
             ref[at, pl.ds(cols, L)] = unpacked(opack_r[0, to, :], opack_r[1, to, :], f)
         return 0
 
-    lax.fori_loop(0, ochunks, ounpack_chunk, 0, unroll=2)
+    lax.fori_loop(0, ochunks, ounpack_chunk, 0, unroll=17)
 
     zero = jnp.zeros((T, L), F32)
 
@@ -750,6 +750,12 @@
     last.wait()
 
 
+def deliver(*refs):
+    half = len(refs) // 2
+    for src, dst in zip(refs[:half], refs[half:]):
+        dst[...] = src[...]
+
+
 def step(groups, tiles, *args):
     base_rhs, thick, ice_vel, ice_stress = args[0], args[5], args[7], args[8]
     orows, cols = base_rhs.shape
@@ -763,7 +769,7 @@
     dma = pltpu.SemaphoreType.DMA
     ice = pltpu.VMEM((2, irows, wide), F32)
     ocean = pltpu.VMEM((erows, wide), F32)
-    return pl.pallas_call(
+    results = pl.pallas_call(
         functools.partial(kernel, groups, tiles),
         out_shape=(
             jax.ShapeDtypeStruct(base_rhs.shape, F32),
@@ -819,6 +825,12 @@
             collective_id=0, has_side_effects=True, vmem_limit_bytes=67_043_328
         ),
     )(*args)
+    return pl.pallas_call(
+        deliver,
+        out_shape=tuple(jax.ShapeDtypeStruct(r.shape, F32) for r in results),
+        in_specs=[vmem] * 3,
+        out_specs=(vmem,) * 3,
+    )(*results)
 
 
 def solution(mesh):

time: 72.5 us -> 69.3 us (0.956)
  local copies, waits for them, and re-layouts: 4.69 us -> 0 us
  Pallas kernels: 66.9 us -> 68.3 us
    unnamed x5 -> x0, local copies, waits for them, and re-layouts: 4.69 us -> none
    pallas_call x0 -> x1, Pallas kernels: none -> 2.71 us  [step(): pl.pallas_call(deliver, out_shape=tuple((jax.ShapeDtypeStruct(r.shape, F3...]
    pallas_call x1, Pallas kernels: 66.9 us -> 65.6 us  [step(): pl.pallas_call(functools.partial(kernel, groups, tiles), out_shape=(jax.S...]
where the time goes in v3:
time: 69.3 us; the launch traced here: 69 us
  Pallas kernels  68.3 us (99%)
    pallas_call x1, Pallas kernels, step(): pl.pallas_call(functools.partial(kernel, groups, tiles), out_shape=(jax.S...  65.6 us
    pallas_call x1, Pallas kernels, step(): pl.pallas_call(deliver, out_shape=tuple((jax.ShapeDtypeStruct(r.shape, F3...  2.71 us

profile of v3, /device:TPU:0, one launch (start us, length us, event | category | flops | bytes accessed | tf_op | source)
XLA Modules:
  0.0 69.0 jit_solution(18355170356246606947)
XLA Ops:
  0.6 65.6 %shard_map.121 = (f32[256,512]{1,0:T(8,128)}, f32[2,2,64,512]{3,2,1,0:T(8,128)}, f32[3,2,64,512]{3,2,1,0:T(8,128)}) custom-call(f32[256,512]{1,0:T(8,128)} %base_in.1, f32[256,512]{1,0:T(8,128)} %depth_in.1, f32[256,512]{1,0:T(8,128)} %ssh_in.1, f32[2,256,512]{2,1,0:T(8,128)} %cur_in.1, s32[32,64]{1,0:T(8,128)} %land_ref.1, f32[2,64,512]{2,1,0:T(8,128)} %thick_in.1, ...), custom_call_target="tpu_custom_call" | custom-call | tf_op jit(solution)/shard_map/pallas_call | solution.py:772
  66.3 2.7 %shard_map.122 = (f32[256,512]{1,0:T(8,128)}, f32[2,2,64,512]{3,2,1,0:T(8,128)}, f32[3,2,64,512]{3,2,1,0:T(8,128)}) custom-call(f32[256,512]{1,0:T(8,128)} %get-tuple-element.6.refs_0_, f32[2,2,64,512]{3,2,1,0:T(8,128)} %get-tuple-element.7.refs_1_, f32[3,2,64,512]{3,2,1,0:T(8,128)} %get-tuple-element.8.refs_2_), custom_call_target="tpu_custom_call" | custom-call | tf_op jit(solution)/shard_map/pallas_call | solution.py:828
